TPU v7x, 512 devices: a whole 4x8x8 slice. The times are simulated.
512 devices in a mesh: ens: 32 (over z_hi, y, core), lat: 4 (over z_lo), lon: 4 (over x).
Axes of the slice: x: 4, y: 8, z: 8 (z_hi: 2, z_lo: 4; z = z_hi * 4 + z_lo), core: 2. Of those that a mesh axis runs over, the one named last changes fastest.
Arguments:
- sample_quantities: bfloat16 [32, 24, 256, 512], P('ens', None, 'lat', 'lon'), may hold values from -6 to 6
- conv_weight: bfloat16 [216, 256], replicated, may hold values from -0.4375 to 0.4375
- conv_bias: float32 [256], replicated, may hold values from -3 to 3
- out_weight: bfloat16 [256, 24], replicated, may hold values from -0.375 to 0.375
- obs_index: int32 [4, 4, 256], P('lat', 'lon'), may hold values from 0 to 196607
- obs_count: int32 [4, 4], P('lat', 'lon'), may hold values from 85 to 256, as said below
- obs_value: float32 [4, 4, 256], P('lat', 'lon'), may hold values from -8 to 8
- obs_weight: float32 [4, 4, 256], P('lat', 'lon'), may hold values from 0.002 to 0.03
Outputs:
- updated_estimates: bfloat16 [32, 24, 256, 512], P('ens', None, 'lat', 'lon')
Inputs may be any that keep to these rules, and one draw needn't show every extreme that they name: `obs_index`: flat index v * 64 * 128 + r * 128 + c into the own shard's block; slots at or past the shard's count are unused. `obs_count`: some shard has exactly 256 live slots.
All inputs are finite; a program needn't handle non-finite values.
Results may differ from a plain program's by a relative error of at most 0.0075.
Values may be sent and summed in bfloat16 or wider, within the bound.
A program may use at most 64 MiB of HBM per device.

v0:
```python
import math

import jax
import jax.numpy as jnp
from jax import lax
from jax.sharding import PartitionSpec as P

NS_ITERS = 20


def extended(shard, sides, width, wrap):
    for axis, dim in sides:
        size, length = (lax.axis_size(axis), shard.shape[dim])
        up = [(i, (i + 1) % size) for i in range(size if wrap else size - 1)]
        down = [(j, i) for i, j in up]
        last = lax.slice_in_dim(shard, length - width, length, axis=dim)
        leading = lax.slice_in_dim(shard, 0, width, axis=dim)
        before = lax.ppermute(last, axis, up)
        after = lax.ppermute(leading, axis, down)
        shard = jnp.concatenate([before, shard, after], axis=dim)
    return shard


def joined_along(parts, dim):
    lengths = list(parts.shape[1:])
    lengths[dim] *= parts.shape[0]
    return jnp.moveaxis(parts, 0, dim).reshape(lengths)


def sent_to_all(shard, axis):
    size = lax.axis_size(axis)
    return lax.all_to_all(
        jnp.broadcast_to(shard[None], (size, *shard.shape)), axis, 0, 0, tiled=True
    )


def collect(shard, axis, dim):
    return joined_along(sent_to_all(shard, axis), dim)


def taken_together(shard, axis):
    everything = sent_to_all(shard, axis)
    return jnp.sum(everything, axis=0)


def together(arrays, axis):
    ends = [0]
    for a in arrays:
        ends.append(ends[-1] + a.size)
    total = taken_together(jnp.concatenate([a.ravel() for a in arrays]), axis)
    return tuple((total[b:e].reshape(a.shape) for a, b, e in zip(arrays, ends, ends[1:])))


def substep(padded, conv_weight, conv_bias, out_weight):
    nvar = padded.shape[0]
    rows = padded.shape[1] - 2
    cols = padded.shape[2] - 2
    patches = jnp.concatenate(
        [padded[:, a : a + rows, b : b + cols] for a in range(3) for b in range(3)], axis=0
    )
    patches = patches.reshape(9 * nvar, rows * cols)
    pre = lax.dot_general(
        conv_weight, patches, (((0,), (0,)), ((), ())), preferred_element_type=jnp.float32
    )
    hidden = jax.nn.gelu(pre + conv_bias[:, None]).astype(jnp.bfloat16)
    change = lax.dot_general(
        out_weight, hidden, (((0,), (0,)), ((), ())), preferred_element_type=jnp.float32
    )
    centre = padded[:, 1:-1, 1:-1].astype(jnp.float32)
    return (centre + change.reshape(nvar, rows, cols)).astype(jnp.bfloat16)


def blend_weights(gram, proj):
    entries_number = gram.shape[0]
    eye = jnp.eye(entries_number, dtype=gram.dtype)
    system = (entries_number - 1) * eye + gram
    scale = jnp.sqrt(jnp.sum(system * system))
    current = system / scale
    inverse = eye
    for turn in range(NS_ITERS):
        factor = 1.5 * eye - 0.5 * jnp.dot(inverse, current, precision=lax.Precision.HIGHEST)
        current = jnp.dot(current, factor, precision=lax.Precision.HIGHEST)
        inverse = jnp.dot(factor, inverse, precision=lax.Precision.HIGHEST)
    root_inv = inverse / jnp.sqrt(scale)
    half = jnp.dot(root_inv, proj, precision=lax.Precision.HIGHEST)
    mean_w = jnp.dot(root_inv, half, precision=lax.Precision.HIGHEST)
    full = mean_w[:, None] + math.sqrt(entries_number - 1.0) * root_inv
    return 1.0 / entries_number + full - jnp.mean(full, axis=0, keepdims=True)


def per_device(
    sample_quantities,
    conv_weight,
    conv_bias,
    out_weight,
    obs_index,
    obs_count,
    obs_value,
    obs_weight,
):
    gridded_quantity = sample_quantities[0]
    nvar, rows, cols = gridded_quantity.shape
    banded = extended(gridded_quantity, (("lat", 1),), 2, False)
    padded = extended(banded, (("lon", 2),), 2, True)
    middle = substep(padded, conv_weight, conv_bias, out_weight)
    total_rows = rows * lax.axis_size("lat")
    global_row = lax.axis_index("lat") * rows - 1 + jnp.arange(rows + 2, dtype=jnp.int32)
    inside = (global_row >= 0) & (global_row < total_rows)
    middle = jnp.where(inside[None, :, None], middle, jnp.zeros_like(middle))
    gridded_quantity = substep(middle, conv_weight, conv_bias, out_weight)
    flat = gridded_quantity.reshape(-1)
    slots = obs_index.reshape(-1)
    picked = jnp.take(flat, slots).astype(jnp.float32)
    members = collect(picked[None, :], "ens", 0)
    live = (jnp.arange(slots.shape[0], dtype=jnp.int32) < obs_count.reshape(())).astype(jnp.float32)
    weight = obs_weight.reshape(-1) * live
    mean = jnp.mean(members, axis=0)
    spread = members - mean[None, :]
    innov = obs_value.reshape(-1) - mean
    weighted = spread * weight[None, :]
    gram_part = jnp.dot(weighted, spread.T, precision=lax.Precision.HIGHEST)
    proj_part = jnp.dot(weighted, innov, precision=lax.Precision.HIGHEST)
    gram, proj = together((gram_part, proj_part), ("lat", "lon"))
    transform_weights_square = blend_weights(gram, proj)
    lanes = gridded_quantity.reshape(1, -1, 128)
    mixed = jnp.einsum(
        "km,krq->mrq",
        transform_weights_square,
        lax.all_to_all(lanes, "ens", split_axis=1, concat_axis=0, tiled=True).astype(jnp.float32),
        precision=lax.Precision.HIGHEST,
    )
    blended = lax.all_to_all(
        mixed.astype(jnp.bfloat16), "ens", split_axis=0, concat_axis=1, tiled=True
    )
    return blended.reshape(1, nvar, rows, cols)


def solution(mesh):
    return jax.shard_map(
        per_device,
        mesh=mesh,
        in_specs=(
            P("ens", None, "lat", "lon"),
            P(),
            P(),
            P(),
            P("lat", "lon", None),
            P("lat", "lon"),
            P("lat", "lon", None),
            P("lat", "lon", None),
        ),
        out_specs=P("ens", None, "lat", "lon"),
        check_vma=False,
    )
```

profile of v0, /device:TPU:1, one launch (start us, length us, event | category | flops | bytes accessed | tf_op | source)
XLA Modules:
  0.0 180.9 jit_solution(248755488847080529)
XLA Ops:
  0.0 0.9 fusion.85
  0.9 4.9 %collective-permute-start = (bf16[24,2,128]{2,1,0:T(2,128)(2,1)S(1)}, bf16[24,2,128]{2,1,0:T(2,128)(2,1)S(1)}, u32[]{:S(2)}, u32[]{:S(2)}) collective-permute-start(bf16[24,2,128]{2,1,0:T(2,128)(2,1)S(1)} %get-tuple-element.11), channel_id=1, source_target_pairs={{0,4},{4,8},{8,12},{1,5},{5,9},{9,13},{2,6},{6,10},{10,14},{3,7},{... | collective-permute-start | bytes 36872 | tf_op jit(solution)/shard_map/ppermute | solution.py:18
  5.9 1.3 collective-permute-start.1
  7.2 0.7 compare_select_fusion
  7.8 3.1 %collective-permute-done.1 = bf16[24,2,128]{2,1,0:T(2,128)(2,1)S(1)} collective-permute-done((bf16[24,2,128]{2,1,0:T(2,128)(2,1)S(1)}, bf16[24,2,128]{2,1,0:T(2,128)(2,1)S(1)}, u32[]{:S(2)}, u32[]{:S(2)}) %collective-permute-start.1) | collective-permute-done | bytes 12320 | tf_op jit(solution)/shard_map/ppermute | solution.py:19
  10.9 1.2 pad_maximum_fusion.2
  12.3 3.1 %collective-permute-start.2 = (bf16[24,68,2]{2,1,0:T(8,128)(2,1)S(1)}, bf16[24,68,2]{2,1,0:T(8,128)(2,1)S(1)}, u32[]{:S(2)}, u32[]{:S(2)}) collective-permute-start(bf16[24,68,2]{2,1,0:T(8,128)(2,1)S(1)} %get-tuple-element.8), channel_id=1, source_target_pairs={{0,1},{1,2},{2,3},{3,0},{4,5},{5,6},{6,7},{7,4},{8,9},{9,10},{10,1... | collective-permute-start | bytes 19592 | tf_op jit(solution)/shard_map/ppermute | solution.py:18
  15.4 3.4 %collective-permute-start.3 = (bf16[24,68,2]{2,1,0:T(8,128)(2,1)S(1)}, bf16[24,68,2]{2,1,0:T(8,128)(2,1)S(1)}, u32[]{:S(2)}, u32[]{:S(2)}) collective-permute-start(bf16[24,68,2]{2,1,0:T(8,128)(2,1)S(1)} %get-tuple-element.7), channel_id=1, source_target_pairs={{1,0},{2,1},{3,2},{0,3},{5,4},{6,5},{7,6},{4,7},{9,8},{10,9},{11,1... | collective-permute-start | bytes 19592 | tf_op jit(solution)/shard_map/ppermute | solution.py:19
  19.5 3.8 %collective-permute-done.2 = bf16[24,68,2]{2,1,0:T(8,128)(2,1)S(1)} collective-permute-done((bf16[24,68,2]{2,1,0:T(8,128)(2,1)S(1)}, bf16[24,68,2]{2,1,0:T(8,128)(2,1)S(1)}, u32[]{:S(2)}, u32[]{:S(2)}) %collective-permute-start.2) | collective-permute-done | bytes 6560 | tf_op jit(solution)/shard_map/ppermute | solution.py:18
  23.3 3.1 %collective-permute-done.3 = bf16[24,68,2]{2,1,0:T(8,128)(2,1)S(1)} collective-permute-done((bf16[24,68,2]{2,1,0:T(8,128)(2,1)S(1)}, bf16[24,68,2]{2,1,0:T(8,128)(2,1)S(1)}, u32[]{:S(2)}, u32[]{:S(2)}) %collective-permute-start.3) | collective-permute-done | bytes 6560 | tf_op jit(solution)/shard_map/ppermute | solution.py:19
  26.4 2.2 %pad_maximum_fusion.1 = (bf16[24,68,130]{2,1,0:T(8,128)(2,1)S(1)}, bf16[24,68,130]{2,1,0:T(8,128)(2,1)S(1)}) fusion(bf16[24,68,2]{2,1,0:T(8,128)(2,1)S(1)} %collective-permute-done.3, bf16[24,2,128]{2,1,0:T(2,128)(2,1)S(1)} %collective-permute-done.1, bf16[24,64,128]{2,1,0:T(8,128)(2,1)} %bitcast.204, bf16[24,2,128]{2,1,0:T(2,128)(2,1)S(1)} %collective-permute-done, ...), kind=kLoop, calls=%fused_computation.85 | loop fusion | flops 3394560 | bytes 1279488 | tf_op jit(solution)/shard_map/concatenate | solution.py:20
  28.7 1.0 slice_dynamic-update-slice_fusion.7
  29.7 0.8 pad_maximum_fusion
  30.4 1.3 slice_dynamic-update-slice_fusion.6
  31.7 1.0 slice_dynamic-update-slice_fusion.5
  32.7 1.3 slice_dynamic-update-slice_fusion.4
  34.0 1.6 slice_dynamic-update-slice_fusion.8
  35.6 1.3 slice_dynamic-update-slice_fusion.3
  36.9 1.3 slice_dynamic-update-slice_fusion.2
  38.3 1.6 slice_dynamic-update-slice_fusion.1
  39.9 1.3 slice_dynamic-update-slice_fusion
  41.2 11.0 %reshape.199 = bf16[216,8580]{1,0:T(8,128)(2,1)} reshape(bf16[216,66,130]{2,1,0:T(8,128)(2,1)} %slice_dynamic-update-slice_fusion) | data formatting | bytes 7413120 | tf_op jit(solution)/shard_map/reshape | solution.py:61
  52.2 5.6 %convolution_bitcast_fusion = f32[24,8580]{1,0:T(8,128)S(1)} fusion(bf16[256,24]{0,1:T(8,128)(2,1)S(1)} %copy-done.6, bf16[216,8580]{1,0:T(8,128)(2,1)} %reshape.199, bf16[216,256]{1,0:T(8,128)(2,1)S(1)} %copy-done, f32[256]{0:T(256)S(1)} %copy-done.7), kind=kOutput, calls=%fused_computation.7 | convolution fusion | flops 1076275200 | bytes 4654144 | tf_op jit(solution)/shard_map/dot_general | solution.py:66
  57.8 2.2 %reshape.172 = f32[24,66,130]{2,1,0:T(8,128)} reshape(f32[24,8580]{1,0:T(8,128)S(1)} %convolution_bitcast_fusion) | data formatting | bytes 1647360 | tf_op jit(solution)/shard_map/reshape | solution.py:70
  60.0 2.2 %fusion.46 = bf16[24,66,130]{2,1,0:T(8,128)(2,1)S(1)} fusion(f32[24,66,130]{2,1,0:T(8,128)} %reshape.172, pred[66]{0:T(512)(128)(4,1)S(1)} %compare_and_fusion, bf16[24,68,132]{2,1,0:T(8,128)(2,1)S(1)} %pad_maximum_fusion), kind=kLoop, calls=%fused_computation.74 | loop fusion | flops 823680 | bytes 1647426 | tf_op jit(solution)/shard_map/jit(_where)/select_n | solution.py:109
  63.1 0.4 slice_dynamic-update-slice_fusion.17
  63.5 0.4 slice_dynamic-update-slice_fusion.12
  64.1 0.4 slice_dynamic-update-slice_fusion.10
  64.6 0.4 slice_dynamic-update-slice_fusion.9
  65.1 1.7 copy-done.2
  66.8 10.4 %fusion.23 = f32[3,8,64,128]{3,1,2,0:T(8,128)S(1)} fusion(bf16[256,24]{0,1:T(8,128)(2,1)S(1)} %copy-done.6, bf16[216,256]{1,0:T(8,128)(2,1)S(1)} %copy-done, f32[256]{0:T(256)S(1)} %copy-done.7, bf16[27,8,64,128]{3,2,1,0:T(8,128)(2,1)} %bitcast.210), kind=kOutput, calls=%fused_computation.28 | convolution fusion | flops 1027604480 | bytes 4449280 | tf_op jit(solution)/shard_map/dot_general | solution.py:66
  77.3 0.4 fusion.47
  77.7 1.9 %gather_fusion = bf16[256]{0:T(256)(128)(2,1)S(1)} fusion(bf16[196608]{0:T(1024)(128)(2,1)S(1)} %bitcast.200, s32[1024]{0:T(1024)S(1)} %pad_clamp_fusion), kind=kCustom, calls=%fused_computation | custom fusion | bytes 2048 | tf_op jit(solution)/shard_map/jit(_take)/gather | solution.py:113
  79.7 0.6 broadcast_in_dim.44
  80.3 17.6 %all-to-all-start = ((f32[32,1,256]{2,1,0:T(1,128)}), f32[32,1,256]{2,1,0:T(1,128)S(1)}, u32[]{:S(2)}, u32[]{:S(2)}) async-start(f32[32,1,256]{2,1,0:T(1,128)} %broadcast_in_dim.44), calls=%async_computation | async-start | bytes 65536 | tf_op jit(solution)/shard_map/all_to_all | solution.py:32
  98.0 11.8 %all-to-all-done = f32[32,1,256]{2,1,0:T(1,128)S(1)} async-done(((f32[32,1,256]{2,1,0:T(1,128)}), f32[32,1,256]{2,1,0:T(1,128)S(1)}, u32[]{:S(2)}, u32[]{:S(2)}) %all-to-all-start) | async-done | bytes 32800 | tf_op jit(solution)/shard_map/all_to_all | solution.py:32
  110.3 0.7 broadcast_in_dim.45
  111.0 5.9 %all-to-all-start.1 = ((f32[16,1,1056]{2,1,0:T(1,128)}), f32[16,1,1056]{2,1,0:T(1,128)S(1)}, u32[]{:S(2)}, u32[]{:S(2)}) async-start(f32[16,1,1056]{2,1,0:T(1,128)} %broadcast_in_dim.45), calls=%async_computation.1 | async-start | bytes 147456 | tf_op jit(solution)/shard_map/all_to_all | solution.py:32
  116.9 6.1 %copy.66 = bf16[1,1536,128]{2,0,1:T(2,128)(2,1)S(1)} copy(bf16[1,1536,128]{2,1,0:T(8,128)(2,1)S(1)} %bitcast.201) | data formatting | bytes 786432 | tf_op jit(solution)/shard_map/reshape | solution.py:125
  123.0 0.5 broadcast.194
  123.6 8.8 %reduce.3 = bf16[1536,128]{1,0:T(8,128)(2,1)S(1)} reduce(bf16[1536,1,128]{2,1,0:T(2,128)(2,1)S(1)} %bitcast.206, bf16[]{:T(256)} %broadcast.194), dimensions={1}, to_apply=%bitcast.198.reduce_sub_computation | reduce | bytes 786434
  132.4 0.8 reshape.200
  133.2 4.7 %all-to-all-start.2 = ((bf16[32,2,3072]{2,1,0:T(2,128)(2,1)}), bf16[32,2,3072]{2,1,0:T(2,128)(2,1)S(1)}, u32[]{:S(2)}, u32[]{:S(2)}) async-start(bf16[32,2,3072]{2,1,0:T(2,128)(2,1)} %reshape.200), calls=%async_computation.2 | async-start | bytes 786432 | tf_op jit(solution)/shard_map/all_to_all | solution.py:129
  138.0 0.7 multiply_reduce_fusion
  148.9 7.1 %all-to-all-done.2 = bf16[32,2,3072]{2,1,0:T(2,128)(2,1)S(1)} async-done(((bf16[32,2,3072]{2,1,0:T(2,128)(2,1)}), bf16[32,2,3072]{2,1,0:T(2,128)(2,1)S(1)}, u32[]{:S(2)}, u32[]{:S(2)}) %all-to-all-start.2) | async-done | bytes 393248 | tf_op jit(solution)/shard_map/all_to_all | solution.py:129
  156.4 0.6 convolution_convert_fusion
  157.2 23.0 %all_to_all.32 = bf16[32,48,128]{2,1,0:T(8,128)(2,1)S(1)} all-to-all(bf16[32,48,128]{2,1,0:T(8,128)(2,1)S(1)} %copy.30), channel_id=1, replica_groups=mesh['ens'=32,'lat'=4,'lon'=4] {'ens'}, dimensions={0} | all-to-all | bytes 786432 | tf_op jit(solution)/shard_map/all_to_all | solution.py:132
  180.2 0.7 copy.85
  (105 shorter events, 11.7 us)
Async XLA Ops:
  0.0 52.2 %copy-start = (bf16[216,256]{1,0:T(8,128)(2,1)S(1)}, bf16[216,256]{1,0:T(8,128)(2,1)}, u32[]{:S(2)}) copy-start(bf16[216,256]{1,0:T(8,128)(2,1)} %param.9) | copy-start | bytes 331780
  0.9 28.8 %copy-start.1 = (bf16[1,24,64,128]{3,2,1,0:T(8,128)(2,1)S(1)}, bf16[1,24,64,128]{3,2,1,0:T(8,128)(2,1)}, u32[]{:S(2)}) copy-start(bf16[1,24,64,128]{3,2,1,0:T(8,128)(2,1)} %param.8) | copy-start | bytes 1179652
  0.9 7.0 %collective-permute-start = (bf16[24,2,128]{2,1,0:T(2,128)(2,1)S(1)}, bf16[24,2,128]{2,1,0:T(2,128)(2,1)S(1)}, u32[]{:S(2)}, u32[]{:S(2)}) collective-permute-start(bf16[24,2,128]{2,1,0:T(2,128)(2,1)S(1)} %get-tuple-element.11), channel_id=1, source_target_pairs={{0,4},{4,8},{8,12},{1,5},{5,9},{9,13},{2,6},{6,10},{10,14},{3,7},{... | collective-permute-start | bytes 36872 | tf_op jit(solution)/shard_map/ppermute | solution.py:18
  5.9 5.1 %collective-permute-start.1 = (bf16[24,2,128]{2,1,0:T(2,128)(2,1)S(1)}, bf16[24,2,128]{2,1,0:T(2,128)(2,1)S(1)}, u32[]{:S(2)}, u32[]{:S(2)}) collective-permute-start(bf16[24,2,128]{2,1,0:T(2,128)(2,1)S(1)} %get-tuple-element.12), channel_id=1, source_target_pairs={{4,0},{8,4},{12,8},{5,1},{9,5},{13,9},{6,2},{10,6},{14,10},{7,3},{... | collective-permute-start | bytes 36872 | tf_op jit(solution)/shard_map/ppermute | solution.py:19
  12.3 11.0 %collective-permute-start.2 = (bf16[24,68,2]{2,1,0:T(8,128)(2,1)S(1)}, bf16[24,68,2]{2,1,0:T(8,128)(2,1)S(1)}, u32[]{:S(2)}, u32[]{:S(2)}) collective-permute-start(bf16[24,68,2]{2,1,0:T(8,128)(2,1)S(1)} %get-tuple-element.8), channel_id=1, source_target_pairs={{0,1},{1,2},{2,3},{3,0},{4,5},{5,6},{6,7},{7,4},{8,9},{9,10},{10,1... | collective-permute-start | bytes 19592 | tf_op jit(solution)/shard_map/ppermute | solution.py:18
  15.4 11.0 %collective-permute-start.3 = (bf16[24,68,2]{2,1,0:T(8,128)(2,1)S(1)}, bf16[24,68,2]{2,1,0:T(8,128)(2,1)S(1)}, u32[]{:S(2)}, u32[]{:S(2)}) collective-permute-start(bf16[24,68,2]{2,1,0:T(8,128)(2,1)S(1)} %get-tuple-element.7), channel_id=1, source_target_pairs={{1,0},{2,1},{3,2},{0,3},{5,4},{6,5},{7,6},{4,7},{9,8},{10,9},{11,1... | collective-permute-start | bytes 19592 | tf_op jit(solution)/shard_map/ppermute | solution.py:19
  41.2 11.0 %copy-start.6 = (bf16[256,24]{0,1:T(8,128)(2,1)S(1)}, bf16[256,24]{0,1:T(8,128)(2,1)}, u32[]{:S(2)}) copy-start(bf16[256,24]{0,1:T(8,128)(2,1)} %param.11) | copy-start | bytes 36868
  41.2 11.0 %copy-start.7 = (f32[256]{0:T(256)S(1)}, f32[256]{0:T(256)}, u32[]{:S(2)}) copy-start(f32[256]{0:T(256)} %param.10) | copy-start | bytes 3076
  65.0 1.8 copy-start.2
  66.8 12.8 %copy-start.3 = (s32[1,1,256]{2,1,0:T(1,128)S(1)}, s32[1,1,256]{2,1,0:T(1,128)}, u32[]{:S(2)}) copy-start(s32[1,1,256]{2,1,0:T(1,128)} %param.12) | copy-start | bytes 3076
  77.2 20.8 %copy-start.5 = (f32[1,1,256]{2,1,0:T(1,128)S(1)}, f32[1,1,256]{2,1,0:T(1,128)}, u32[]{:S(2)}) copy-start(f32[1,1,256]{2,1,0:T(1,128)} %param.15) | copy-start | bytes 3076
  77.2 33.0 %copy-start.4 = (f32[1,1,256]{2,1,0:T(1,128)S(1)}, f32[1,1,256]{2,1,0:T(1,128)}, u32[]{:S(2)}) copy-start(f32[1,1,256]{2,1,0:T(1,128)} %param.14) | copy-start | bytes 3076
  80.3 29.5 %all-to-all-start = ((f32[32,1,256]{2,1,0:T(1,128)}), f32[32,1,256]{2,1,0:T(1,128)S(1)}, u32[]{:S(2)}, u32[]{:S(2)}) async-start(f32[32,1,256]{2,1,0:T(1,128)} %broadcast_in_dim.44), calls=%async_computation | async-start | bytes 65536 | tf_op jit(solution)/shard_map/all_to_all | solution.py:32
  111.0 22.2 %all-to-all-start.1 = ((f32[16,1,1056]{2,1,0:T(1,128)}), f32[16,1,1056]{2,1,0:T(1,128)S(1)}, u32[]{:S(2)}, u32[]{:S(2)}) async-start(f32[16,1,1056]{2,1,0:T(1,128)} %broadcast_in_dim.45), calls=%async_computation.1 | async-start | bytes 147456 | tf_op jit(solution)/shard_map/all_to_all | solution.py:32
  133.2 22.8 %all-to-all-start.2 = ((bf16[32,2,3072]{2,1,0:T(2,128)(2,1)}), bf16[32,2,3072]{2,1,0:T(2,128)(2,1)S(1)}, u32[]{:S(2)}, u32[]{:S(2)}) async-start(bf16[32,2,3072]{2,1,0:T(2,128)(2,1)} %reshape.200), calls=%async_computation.2 | async-start | bytes 786432 | tf_op jit(solution)/shard_map/all_to_all | solution.py:129
where the time goes:
time: 183 us; the launch traced here: 181 us
  local copies, waits for them, and re-layouts  42.9 us (23%)
  starting transfers between devices  41 us (22%)
  waiting for transfers between devices  29 us (16%)
  matrix products  25.9 us (14%)
  blocking collectives  23 us (13%)
  other arithmetic  17.2 us (9%)
  between operations  1.98 us (1%)
    all_to_all x2, starting transfers between devices, sent_to_all(): lax.all_to_all(jnp.broadcast_to(shard[None], (size, *shard.shape)), axis,...  23.5 us
    all_to_all x1, blocking collectives, per_device(): lax.all_to_all(mixed.astype(jnp.bfloat16), 'ens', split_axis=0, concat_ax...  23 us
    unnamed x38, local copies, waits for them, and re-layouts  17.1 us
    dot_general x2, matrix products, substep(): lax.dot_general(out_weight, hidden, (((0,), (0,)), ((), ())), preferred_e...  16 us
    all_to_all x2, waiting for transfers between devices, sent_to_all(): lax.all_to_all(jnp.broadcast_to(shard[None], (size, *shard.shape)), axis,...  11.8 us
    reshape x1, local copies, waits for them, and re-layouts, substep(): patches = patches.reshape(9 * nvar, rows * cols)  11 us
    unnamed x1, other arithmetic  8.8 us
    ppermute x2, starting transfers between devices, extended(): before = lax.ppermute(last, axis, up)  8.07 us
  transfers between devices with their start and end apart: 7, of which 5 were waited for; matrix products, arithmetic and copies ran while one was open for 15% of the time, Pallas kernels for 0%

commit v1 on v0

v1 whole, which is shorter than its diff:
```python
import math

import jax
import jax.numpy as jnp
from jax import lax
from jax.experimental import pallas as pl
from jax.experimental.pallas import tpu as pltpu
from jax.sharding import PartitionSpec as P

NS_ITERS = 20
MESH = pl.DeviceIdType.MESH
F32 = jnp.float32
BF16 = jnp.bfloat16
NV = 24
ROWS = 64
LANES = 128
SLAB = 80
NE = 32
NA = 4
NB = 4
PITCH = 72
NOBS = 256


def dot(a, b, dims=((1,), (0,)), precision=None):
    return lax.dot_general(
        a, b, (dims, ((), ())), precision=precision, preferred_element_type=F32
    )


def marks(hit):
    return jnp.where(hit, 1.0, 0.0).astype(BF16)


def lane_iota(shape):
    return lax.broadcasted_iota(jnp.int32, shape, len(shape) - 1)


def row_iota(shape):
    return lax.broadcasted_iota(jnp.int32, shape, len(shape) - 2)


def roll(x, shift):
    if isinstance(shift, int):
        shift = shift % LANES
        if shift == 0:
            return x
    return pltpu.roll(x, shift, 1)


def slab(x, west, east):
    lane = lane_iota((NV, LANES))
    xw = jnp.where(lane == 0, west, roll(x, 1))
    xe = jnp.where(lane == LANES - 1, east, roll(x, -1))
    return jnp.concatenate([xw, x, xe, jnp.ones((8, LANES), F32)], axis=0).astype(BF16)


def gelu2(pre):
    c1 = math.sqrt(2.0 / math.pi)
    c2 = c1 * 0.044715
    th = jnp.tanh(pre * (c1 + c2 * (pre * pre)))
    return (pre + pre * th).astype(BF16)


def changes(wt, ow, patches):
    pre = dot(wt, patches)
    return dot(ow, gelu2(pre))


def kernel(
    x_hbm, cw_hbm, cb_hbm, ow_hbm, oi_hbm, oc_hbm, ov_hbm, og_hbm, out_ref,
    xv, cw, cb, ow, oi, oc, ov, og,
    big, s1, s2, wt, owt, hrow_s, hcol_s, hrow, hcol, obs_s, obs_r,
    fc, recv, back, res, pick_s, hx, gsend, grecv, acc, ep, oh, sp, ets,
    load_sem, hsend, hrecv, asend, arecv, psend, precv, gsend_sem, grecv_sem,
    bsend, brecv,
):
    k = lax.axis_index("ens")
    i = lax.axis_index("lat")
    j = lax.axis_index("lon")
    i2 = (i + 2) % NA
    k_hi, k_y, k_c = k // 16, (k // 2) % 8, k % 2

    def peer(dk, di, dj):
        return ((k + dk) % NE, (i + di) % NA, (j + dj) % NB)

    def partner(s):
        u = s // 4
        dy = ((u + 1) // 2) * (2 * (u % 2) - 1)
        hi = (k_hi + s) % 2
        y = (k_y + 8 + dy) % 8
        c = (k_c + s // 2) % 2
        return hi * 16 + y * 2 + c

    barrier = pltpu.get_barrier_semaphore()
    for di in range(NA):
        for dj in range(NB):
            if di or dj:
                pl.semaphore_signal(
                    barrier, inc=1, device_id=peer(0, di, dj), device_id_type=MESH
                )
    for dk in range(1, NE):
        pl.semaphore_signal(barrier, inc=1, device_id=peer(dk, 2, 0), device_id_type=MESH)

    loads = [
        pltpu.make_async_copy(src, dst, load_sem.at[n])
        for n, (src, dst) in enumerate(
            [(x_hbm, xv), (cw_hbm, cw), (cb_hbm, cb), (ow_hbm, ow),
             (oi_hbm, oi), (oc_hbm, oc), (ov_hbm, ov), (og_hbm, og)]
        )
    ]
    for c in loads:
        c.start()
    for c in loads:
        c.wait()

    lane24 = lane_iota((NV, LANES))

    for v in range(NV):
        big[v * PITCH : v * PITCH + ROWS, :] = xv[0, v].astype(F32)

    def row_of(r):
        return big[pl.ds(r, NV, stride=PITCH), :]

    def extract(r4, cols):
        for q in range(4):
            r = r4 * 4 + q
            x = roll(row_of(r), r)
            cols = tuple(
                jnp.where(lane24 == (r + off) % LANES, x, c)
                for c, off in zip(cols, (0, 1, LANES - 2, LANES - 1))
            )
        return cols

    zero24 = jnp.zeros((NV, LANES), F32)
    c0, c1, c126, c127 = lax.fori_loop(0, ROWS // 4, extract, (zero24,) * 4)
    c1 = roll(c1, -1)
    c126 = roll(c126, 2)
    c127 = roll(c127, 1)
    hcol_s[0] = jnp.concatenate([c0, c1], axis=0).astype(BF16)
    hcol_s[1] = jnp.concatenate([c126, c127], axis=0).astype(BF16)
    hrow_s[0] = jnp.concatenate([row_of(0), row_of(1)], axis=0).astype(BF16)
    hrow_s[1] = jnp.concatenate([row_of(ROWS - 2), row_of(ROWS - 1)], axis=0).astype(BF16)
    live = (lane_iota((1, NOBS)) < oc[...]).astype(F32)
    obs_s[0:1, :] = ov[0]
    obs_s[1:2, :] = og[0] * live
    obs_s[2:8, :] = jnp.zeros((6, NOBS), F32)

    pl.semaphore_wait(barrier, NA * NB - 1 + NE - 1)

    def halo(src, dst, n, di, dj):
        return pltpu.make_async_remote_copy(
            src_ref=src, dst_ref=dst, send_sem=hsend.at[n], recv_sem=hrecv.at[n],
            device_id=peer(0, di, dj), device_id_type=MESH,
        )

    north = [
        halo(hrow_s.at[1], hrow.at[0], 0, 1, 0),
        halo(hcol_s.at[1], hcol.at[2], 4, 1, 1),
        halo(hcol_s.at[0], hcol.at[3], 5, 1, -1),
    ]
    south = [
        halo(hrow_s.at[0], hrow.at[1], 1, -1, 0),
        halo(hcol_s.at[1], hcol.at[4], 6, -1, 1),
        halo(hcol_s.at[0], hcol.at[5], 7, -1, -1),
    ]
    sides = [
        halo(hcol_s.at[1], hcol.at[0], 2, 0, 1),
        halo(hcol_s.at[0], hcol.at[1], 3, 0, -1),
    ]
    obs_copy = halo(obs_s, obs_r, 8, 2, 0)

    @pl.when(i < NA - 1)
    def _():
        for c in north:
            c.start()

    @pl.when(i > 0)
    def _():
        for c in south:
            c.start()

    for c in sides:
        c.start()
    obs_copy.start()

    @pl.when(i == 0)
    def _():
        hrow[0] = jnp.zeros((2 * NV, LANES), BF16)
        hcol[2] = jnp.zeros((2 * NV, LANES), BF16)
        hcol[3] = jnp.zeros((2 * NV, LANES), BF16)

    @pl.when(i == NA - 1)
    def _():
        hrow[1] = jnp.zeros((2 * NV, LANES), BF16)
        hcol[4] = jnp.zeros((2 * NV, LANES), BF16)
        hcol[5] = jnp.zeros((2 * NV, LANES), BF16)

    w = cw[...].astype(F32)
    b = cb[...]
    b_hi = b.astype(BF16).astype(F32)
    b_mid = (b - b_hi).astype(BF16).astype(F32)
    b_lo = b - b_hi - b_mid
    zeros8 = jnp.zeros((8, 256), F32)
    pad = row_iota((8, 256))
    bias8 = jnp.where(pad == 0, b_hi, jnp.where(pad == 1, b_mid, jnp.where(pad == 2, b_lo, zeros8)))
    wfull = jnp.concatenate(
        [w[0:72], bias8, w[72:144], zeros8, w[144:216], zeros8, zeros8, zeros8], axis=0
    )
    wt[...] = wfull.T.astype(BF16)
    owp = jnp.concatenate([ow[...].astype(F32) * 0.5, jnp.zeros((256, 104), F32)], axis=1)
    owt[...] = owp.T[0:32].astype(BF16)
    tail = jnp.zeros((16, LANES), BF16)
    s1[68 * SLAB : 68 * SLAB + 16, :] = tail
    s2[66 * SLAB : 66 * SLAB + 16, :] = tail

    for c in sides:
        c.wait()
    obs_copy.wait()

    @pl.when(i > 0)
    def _():
        for c in north:
            c.wait_recv()

    @pl.when(i < NA - 1)
    def _():
        for c in north:
            c.wait_send()
        for c in south:
            c.wait_recv()

    @pl.when(i > 0)
    def _():
        for c in south:
            c.wait_send()

    def pair(ref, n):
        both = ref[n].astype(F32)
        return both[0:NV], both[NV : 2 * NV]

    n0, n1 = pair(hrow, 0)
    m0, m1 = pair(hrow, 1)

    def ext(mid, top, bottom):
        out = roll(mid, 2)
        out = jnp.where(lane24 < 2, roll(top, 2 - ROWS), out)
        return jnp.where(lane24 > ROWS + 1, roll(bottom, ROWS + 2), out)

    w_m, w_n, w_s = pair(hcol, 0), pair(hcol, 2), pair(hcol, 4)
    e_m, e_n, e_s = pair(hcol, 1), pair(hcol, 3), pair(hcol, 5)
    cm2 = ext(w_m[0], w_n[0], w_s[0])
    cm1 = ext(w_m[1], w_n[1], w_s[1])
    cp0 = ext(e_m[0], e_n[0], e_s[0])
    cp1 = ext(e_m[1], e_n[1], e_s[1])

    def own(mid, lane):
        out = roll(mid, 2)
        for at, x in ((0, n0), (1, n1), (ROWS + 2, m0), (ROWS + 3, m1)):
            out = jnp.where(lane24 == at, roll(x, at - lane), out)
        return out

    c0e = own(c0, 0)
    c127e = own(c127, LANES - 1)

    def put1(n, x):
        s1[pl.ds(pl.multiple_of(n * SLAB, 16), SLAB), :] = slab(
            x, roll(cm1, (LANES - n) % LANES), roll(cp0, (2 * LANES - 1 - n) % LANES)
        )

    for n, x in ((0, n0), (1, n1), (ROWS + 2, m0), (ROWS + 3, m1)):
        put1(n, x)

    def build(r4, carry):
        for q in range(4):
            r = r4 * 4 + q
            put1(r + 2, row_of(r))
        return carry

    lax.fori_loop(0, ROWS // 4, build, 0)

    weights = wt[...]
    oweights = owt[...]

    def edge(a0, a1, a2):
        ones = jnp.ones((8, LANES), F32)
        rows = []
        for a in range(3):
            rows += [roll(a0, -a), roll(a1, -a), roll(a2, -a), ones]
        rows.append(jnp.zeros((16, LANES), F32))
        return jnp.concatenate(rows, axis=0).astype(BF16)

    first, last = i > 0, i < NA - 1
    ep[:, 0:LANES] = edge(cm2, cm1, c0e)
    ep[:, LANES : 2 * LANES] = edge(c127e, cp0, cp1)
    ch = changes(weights, oweights, ep[...])
    inside = ((lane24 > 0) | first) & ((lane24 < ROWS + 1) | last)
    mw = jnp.where(inside, roll(cm1, -1) + ch[0:NV, 0:LANES], 0.0)
    me = jnp.where(inside, roll(cp0, -1) + ch[0:NV, LANES : 2 * LANES], 0.0)

    def tile(s, n):
        base = pl.multiple_of(n * SLAB, 16)
        p = jnp.concatenate([s[pl.ds(base, 256), :], s[pl.ds(base + SLAB, 256), :]], axis=1)
        c = changes(weights, oweights, p)
        mid0 = s[pl.ds(base + SLAB, SLAB), :].astype(F32)[NV : 2 * NV]
        mid1 = s[pl.ds(base + 2 * SLAB, SLAB), :].astype(F32)[NV : 2 * NV]
        return mid0 + c[0:NV, 0:LANES], mid1 + c[0:NV, LANES : 2 * LANES]

    def step1(t3, carry):
        for q in range(3):
            n = (t3 * 3 + q) * 2
            for d, m in enumerate(tile(s1, n)):
                at = n + d
                keep = ((at > 0) | first) & ((at < ROWS + 1) | last)
                m = jnp.where(keep, m, 0.0)
                s2[pl.ds(pl.multiple_of(at * SLAB, 16), SLAB), :] = slab(
                    m,
                    roll(mw, (LANES - at) % LANES),
                    roll(me, (2 * LANES - 1 - at) % LANES),
                )
        return carry

    lax.fori_loop(0, 11, step1, 0)

    flat = oi[0]
    v_of, r_of, c_of = flat // 8192, (flat // LANES) % ROWS, flat % LANES
    where_row = r_of * NV + v_of
    oh[...] = marks(row_iota((LANES, NOBS)) == c_of)
    acc[...] = jnp.zeros((8, NOBS), F32)

    def send_tile(s):
        t = partner(s)
        return pltpu.make_async_remote_copy(
            src_ref=fc.at[t], dst_ref=recv.at[k], send_sem=asend.at[t], recv_sem=arecv.at[k],
            device_id=(t, i2, j), device_id_type=MESH,
        )

    def step2(s2i, carry):
        for q in range(2):
            t = partner(s2i * 2 + q)
            f0, f1 = tile(s2, t * 2)
            f = jnp.concatenate([f0, f1], axis=0).astype(BF16)
            fc[t] = f
            at_c = dot(f, oh[...])
            hit = row_iota((2 * NV, NOBS)) + t * (2 * NV) == where_row
            sel = jnp.where(hit, at_c, 0.0)
            total = sel[0:8]
            for g in range(1, 6):
                total = total + sel[8 * g : 8 * g + 8]
            acc[...] += total
        return carry

    lax.fori_loop(0, NE // 2, step2, 0)

    pick_s[0] = jnp.sum(acc[...], axis=0, keepdims=True)

    def send_pick(t):
        return pltpu.make_async_remote_copy(
            src_ref=pick_s.at[0], dst_ref=hx.at[k], send_sem=psend.at[t], recv_sem=precv.at[k],
            device_id=(t, i2, j), device_id_type=MESH,
        )

    def over(n, body):
        lax.fori_loop(0, n, lambda s, c: (body(s), c)[1], 0)

    over(NE, lambda s: send_pick(partner(s)).start())
    over(NE, lambda s: send_tile(s).start())

    def recv_pick(t):
        return pltpu.make_async_remote_copy(
            src_ref=pick_s.at[0], dst_ref=hx.at[t], send_sem=psend.at[t], recv_sem=precv.at[t],
            device_id=(t, i2, j), device_id_type=MESH,
        )

    over(NE, lambda t: recv_pick(t).wait_recv())

    values = hx[:, 0, :]
    value = obs_r[0:1, :]
    weight = obs_r[1:2, :]
    mean = jnp.mean(values, axis=0, keepdims=True)
    dev = values - mean
    innov = value - mean
    rows40 = jnp.concatenate([dev, jnp.broadcast_to(innov, (8, NOBS))], axis=0)
    wdev = dev * weight
    hp = lax.Precision.HIGHEST
    g4 = dot(rows40, jnp.concatenate([wdev] * 4, axis=0), ((1,), (1,)), hp)
    lane8 = lane_iota((8, LANES))
    packed = jnp.zeros((8, LANES), F32)
    for q in range(4):
        packed = jnp.where(lane8 // 32 == q, g4[8 * q : 8 * q + 8], packed)
    mine = jnp.concatenate([packed, g4[32:40]], axis=0)
    gsend[...] = mine
    slot = i * NB + j
    grecv[slot] = mine

    def send_gram(di, dj):
        n = (di % NA) * NB + dj % NB
        return pltpu.make_async_remote_copy(
            src_ref=gsend, dst_ref=grecv.at[slot], send_sem=gsend_sem.at[n],
            recv_sem=grecv_sem.at[slot], device_id=peer(0, di, dj), device_id_type=MESH,
        )

    def recv_gram(di, dj):
        n = ((i + di) % NA) * NB + (j + dj) % NB
        return pltpu.make_async_remote_copy(
            src_ref=gsend, dst_ref=grecv.at[n], send_sem=gsend_sem.at[0],
            recv_sem=grecv_sem.at[n], device_id=peer(0, di, dj), device_id_type=MESH,
        )

    others = [(di, dj) for di in range(NA) for dj in range(NB) if di or dj]
    for di, dj in others:
        send_gram(di, dj).start()
    for di, dj in others:
        recv_gram(di, dj).wait_recv()

    total = grecv[0]
    for n in range(1, NA * NB):
        total = total + grecv[n]
    p1, p2 = total[0:8], total[8:16]
    gram = jnp.concatenate(
        [(p1 if q == 0 else roll(p1, -32 * q))[:, 0:32] for q in range(4)], axis=0
    )
    proj = p2[:, 0:32]
    eye = jnp.where(row_iota((NE, NE)) == lane_iota((NE, NE)), 1.0, 0.0)
    system = (NE - 1) * eye + gram

    def full_sum(a):
        return jnp.sum(jnp.sum(a, axis=1, keepdims=True), axis=0, keepdims=True)

    scale = jnp.sqrt(full_sum(system * system))

    current, inverse = system / scale, eye
    for _ in range(NS_ITERS):
        factor = 1.5 * eye - 0.5 * dot(inverse, current, precision=hp)
        new = dot(jnp.concatenate([current, inverse], axis=0), factor, precision=hp)
        current, inverse = new[0:NE], new[NE : 2 * NE]
    root = inverse / jnp.sqrt(scale)
    half = dot(proj, root, precision=hp)
    mean_w = dot(half, root, precision=hp)[0:1]
    full = mean_w + math.sqrt(NE - 1.0) * root
    et = 1.0 / NE + full - jnp.mean(full, axis=1, keepdims=True)
    et_hi = et.astype(BF16)
    et_lo = (et - et_hi.astype(F32)).astype(BF16)

    spread = marks(row_iota((512, NE)) // 16 == lane_iota((512, NE)))
    sp[...] = marks(row_iota((NE, 512)) == lane_iota((NE, 512)) // 16)
    ets[0] = et_hi
    ets[1] = et_lo
    same = row_iota((512, 512)) % 16 == lane_iota((512, 512)) % 16

    def kron(e):
        a = dot(spread, e).astype(BF16)
        return jnp.where(same, dot(a, sp[...]), 0.0).astype(BF16)

    kr_hi = kron(ets[0])
    kr_lo = kron(ets[1])

    def recv_tile(t):
        return pltpu.make_async_remote_copy(
            src_ref=fc.at[t], dst_ref=recv.at[t], send_sem=asend.at[t], recv_sem=arecv.at[t],
            device_id=(t, i2, j), device_id_type=MESH,
        )

    over(NE, lambda t: recv_tile(t).wait_recv())

    for q in range(3):
        f = recv[:, 16 * q : 16 * q + 16, :].reshape(512, LANES)
        o = dot(kr_hi, f) + dot(kr_lo, f)
        back[:, 16 * q : 16 * q + 16, :] = o.astype(BF16).reshape(NE, 16, LANES)

    def send_back(s):
        t = partner(s)
        return pltpu.make_async_remote_copy(
            src_ref=back.at[t], dst_ref=res.at[k], send_sem=bsend.at[t], recv_sem=brecv.at[k],
            device_id=(t, i2, j), device_id_type=MESH,
        )

    def recv_back(t):
        return pltpu.make_async_remote_copy(
            src_ref=back.at[t], dst_ref=res.at[t], send_sem=bsend.at[t], recv_sem=brecv.at[t],
            device_id=(t, i2, j), device_id_type=MESH,
        )

    over(NE, lambda s: send_back(s).start())

    def finish(t):
        recv_back(t).wait_recv()
        big[pl.ds(pl.multiple_of(t * 48, 16), 48), :] = res[t].astype(F32)

    over(NE, finish)
    for v in range(NV):
        out_ref[0, v] = big[pl.ds(v, ROWS, stride=NV), :].astype(BF16)

    over(NE, lambda t: recv_pick(t).wait_send())
    over(NE, lambda t: recv_tile(t).wait_send())
    over(NE, lambda t: recv_back(t).wait_send())
    for di, dj in others:
        send_gram(di, dj).wait_send()


def per_device(x, cw, cb, ow, oi, oc, ov, og):
    anyspec = pl.BlockSpec(memory_space=pl.ANY)
    return pl.pallas_call(
        kernel,
        out_shape=jax.ShapeDtypeStruct(x.shape, x.dtype),
        in_specs=[anyspec] * 8,
        out_specs=pl.BlockSpec(memory_space=pltpu.VMEM),
        scratch_shapes=[
            pltpu.VMEM(x.shape, BF16),
            pltpu.VMEM(cw.shape, BF16),
            pltpu.VMEM((1, 256), F32),
            pltpu.VMEM(ow.shape, BF16),
            pltpu.VMEM((1, 1, NOBS), jnp.int32),
            pltpu.VMEM((1, 1), jnp.int32),
            pltpu.VMEM((1, 1, NOBS), F32),
            pltpu.VMEM((1, 1, NOBS), F32),
            pltpu.VMEM((NV * PITCH, LANES), F32),
            pltpu.VMEM((68 * SLAB + 16, LANES), BF16),
            pltpu.VMEM((66 * SLAB + 16, LANES), BF16),
            pltpu.VMEM((256, 256), BF16),
            pltpu.VMEM((32, 256), BF16),
            pltpu.VMEM((2, 2 * NV, LANES), BF16),
            pltpu.VMEM((2, 2 * NV, LANES), BF16),
            pltpu.VMEM((2, 2 * NV, LANES), BF16),
            pltpu.VMEM((6, 2 * NV, LANES), BF16),
            pltpu.VMEM((8, NOBS), F32),
            pltpu.VMEM((8, NOBS), F32),
            pltpu.VMEM((NE, 2 * NV, LANES), BF16),
            pltpu.VMEM((NE, 2 * NV, LANES), BF16),
            pltpu.VMEM((NE, 2 * NV, LANES), BF16),
            pltpu.VMEM((NE, 2 * NV, LANES), BF16),
            pltpu.VMEM((1, 1, NOBS), F32),
            pltpu.VMEM((NE, 1, NOBS), F32),
            pltpu.VMEM((16, LANES), F32),
            pltpu.VMEM((NA * NB, 16, LANES), F32),
            pltpu.VMEM((8, NOBS), F32),
            pltpu.VMEM((256, 256), BF16),
            pltpu.VMEM((LANES, NOBS), BF16),
            pltpu.VMEM((NE, 512), BF16),
            pltpu.VMEM((2, NE, NE), BF16),
            pltpu.SemaphoreType.DMA((8,)),
            pltpu.SemaphoreType.DMA((9,)),
            pltpu.SemaphoreType.DMA((9,)),
            pltpu.SemaphoreType.DMA((NE,)),
            pltpu.SemaphoreType.DMA((NE,)),
            pltpu.SemaphoreType.DMA((NE,)),
            pltpu.SemaphoreType.DMA((NE,)),
            pltpu.SemaphoreType.DMA((NA * NB,)),
            pltpu.SemaphoreType.DMA((NA * NB,)),
            pltpu.SemaphoreType.DMA((NE,)),
            pltpu.SemaphoreType.DMA((NE,)),
        ],
        compiler_params=pltpu.CompilerParams(
            collective_id=0, has_side_effects=True, vmem_limit_bytes=48 * 1024 * 1024
        ),
        name="cycle",
    )(x, cw, cb.reshape(1, 256), ow, oi, oc, ov, og)


def solution(mesh):
    return jax.shard_map(
        per_device,
        mesh=mesh,
        in_specs=(
            P("ens", None, "lat", "lon"),
            P(),
            P(),
            P(),
            P("lat", "lon", None),
            P("lat", "lon"),
            P("lat", "lon", None),
            P("lat", "lon", None),
        ),
        out_specs=P("ens", None, "lat", "lon"),
        check_vma=False,
    )
```

time: 183 us -> 92.1 us (0.50)
  Pallas kernels: 0 us -> 87.6 us
  starting transfers between devices: 41 us -> 0 us
  local copies, waits for them, and re-layouts: 42.9 us -> 3.5 us
  waiting for transfers between devices: 29 us -> 0 us
  matrix products: 25.9 us -> 0 us
  blocking collectives: 23 us -> 0 us
  other arithmetic: 17.2 us -> 0 us
    pallas_call x0 -> x1, Pallas kernels: none -> 87.6 us  [per_device(): pl.pallas_call(kernel, out_shape=jax.ShapeDtypeStruct(x.shape, x.dtype),...]
    all_to_all x3 -> x0, starting transfers between devices: 28.2 us -> none  [the longest x2 23.5 us: sent_to_all(): lax.all_to_all(jnp.broadcast_to(shard[None], (size, *shard.shape)), axis,...]
    dot_general x66 -> x0, matrix products: 25.9 us -> none  [the longest x2 16 us: substep(): lax.dot_general(out_weight, hidden, (((0,), (0,)), ((), ())), preferred_e...]
    all_to_all x1 -> x0, blocking collectives: 23 us -> none  [per_device(): lax.all_to_all(mixed.astype(jnp.bfloat16), 'ens', split_axis=0, concat_ax...]
    reshape x5 -> x0, local copies, waits for them, and re-layouts: 19.5 us -> none  [the longest x1 11 us: substep(): patches = patches.reshape(9 * nvar, rows * cols)]
    all_to_all x3 -> x0, waiting for transfers between devices: 19 us -> none  [the longest x2 11.8 us: sent_to_all(): lax.all_to_all(jnp.broadcast_to(shard[None], (size, *shard.shape)), axis,...]
    unnamed x38 -> x14, local copies, waits for them, and re-layouts: 17.1 us -> 3.5 us
    ppermute x4 -> x0, starting transfers between devices: 12.7 us -> none  [the longest x2 8.07 us: extended(): before = lax.ppermute(last, axis, up)]
  transfers between devices with their start and end apart: 7 -> 0, of which waited for: 5 -> 0; matrix products, arithmetic and copies ran while one was open for 15% -> 0% of each run, Pallas kernels for 0% -> 0%
where the time goes in v1:
time: 92.1 us; the launch traced here: 91.8 us
  Pallas kernels  87.6 us (95%)
  local copies, waits for them, and re-layouts  3.5 us (4%)
    pallas_call x1, Pallas kernels, per_device(): pl.pallas_call(kernel, out_shape=jax.ShapeDtypeStruct(x.shape, x.dtype),...  87.6 us
    unnamed x14, local copies, waits for them, and re-layouts  3.5 us

profile of v1, /device:TPU:1, one launch (start us, length us, event | category | flops | bytes accessed | tf_op | source)
XLA Modules:
  0.0 91.8 jit_solution(10586346156105097538)
XLA Ops:
  0.7 0.0 copy-start.2
  0.7 0.0 copy-start.3
  0.7 0.0 copy-start.4
  0.7 0.0 copy-start.5
  0.7 0.8 copy.9.ow_hbm
  1.5 0.0 copy-done.2
  1.5 0.0 copy-done.3
  1.6 0.0 copy-done.4
  1.6 0.0 copy-done.5
  1.6 0.0 copy-start
  1.6 1.0 %copy-done = bf16[1,24,64,128]{3,2,1,0:T(8,128)(2,1)S(1)} copy-done((bf16[1,24,64,128]{3,2,1,0:T(8,128)(2,1)S(1)}, bf16[1,24,64,128]{3,2,1,0:T(8,128)(2,1)}, u32[]{:S(2)}) %copy-start) | copy-done | bytes 393240
  2.6 0.0 copy-start.1
  2.6 0.9 copy-done.1
  3.5 87.6 %cycle.1 = bf16[1,24,64,128]{3,2,1,0:T(8,128)(2,1)S(1)} custom-call(bf16[1,24,64,128]{3,2,1,0:T(8,128)(2,1)S(1)} %copy-done, bf16[216,256]{1,0:T(8,128)(2,1)S(1)} %copy-done.1, f32[1,256]{1,0:T(1,128)S(1)} %bitcast.1, bf16[256,24]{1,0:T(8,128)(2,1)S(1)} %copy.9.ow_hbm, s32[1,1,256]{2,1,0:T(1,128)S(1)} %copy-done.3, s32[1,1]{1,0:T(1,128)S(6)} %copy.11.oc_hbm, ...), custom_call_target="tpu_custom_call" | custom-call | tf_op jit(solution)/shard_map/cycle/pallas_call | solution.py:503
  91.1 0.7 copy.12
Async XLA Ops:
  0.7 0.9 copy-start.2
  0.7 0.9 copy-start.3
  0.7 0.9 copy-start.4
  0.7 0.9 copy-start.5
  1.6 1.0 %copy-start = (bf16[1,24,64,128]{3,2,1,0:T(8,128)(2,1)S(1)}, bf16[1,24,64,128]{3,2,1,0:T(8,128)(2,1)}, u32[]{:S(2)}) copy-start(bf16[1,24,64,128]{3,2,1,0:T(8,128)(2,1)} %x_hbm.1) | copy-start | bytes 1179652
  2.6 0.9 copy-start.1

commit v2 on v1

--- a/solution.py
+++ b/solution.py
@@ -58,8 +58,9 @@
 def gelu2(pre):
     c1 = math.sqrt(2.0 / math.pi)
     c2 = c1 * 0.044715
-    th = jnp.tanh(pre * (c1 + c2 * (pre * pre)))
-    return (pre + pre * th).astype(BF16)
+    x = pre.astype(BF16)
+    th = jnp.tanh(x * (jnp.bfloat16(c1) + jnp.bfloat16(c2) * (x * x)))
+    return x + x * th
 
 
 def changes(wt, ow, patches):
@@ -92,6 +93,16 @@
         c = (k_c + s // 2) % 2
         return hi * 16 + y * 2 + c
 
+    loads = [
+        pltpu.make_async_copy(src, dst, load_sem.at[n])
+        for n, (src, dst) in enumerate(
+            [(x_hbm, xv), (cw_hbm, cw), (cb_hbm, cb), (ow_hbm, ow),
+             (oi_hbm, oi), (oc_hbm, oc), (ov_hbm, ov), (og_hbm, og)]
+        )
+    ]
+    for c in loads:
+        c.start()
+
     barrier = pltpu.get_barrier_semaphore()
     for di in range(NA):
         for dj in range(NB):
@@ -102,15 +113,6 @@
     for dk in range(1, NE):
         pl.semaphore_signal(barrier, inc=1, device_id=peer(dk, 2, 0), device_id_type=MESH)
 
-    loads = [
-        pltpu.make_async_copy(src, dst, load_sem.at[n])
-        for n, (src, dst) in enumerate(
-            [(x_hbm, xv), (cw_hbm, cw), (cb_hbm, cb), (ow_hbm, ow),
-             (oi_hbm, oi), (oc_hbm, oc), (ov_hbm, ov), (og_hbm, og)]
-        )
-    ]
-    for c in loads:
-        c.start()
     for c in loads:
         c.wait()
 
@@ -122,18 +124,15 @@
     def row_of(r):
         return big[pl.ds(r, NV, stride=PITCH), :]
 
-    def extract(r4, cols):
-        for q in range(4):
-            r = r4 * 4 + q
-            x = roll(row_of(r), r)
-            cols = tuple(
-                jnp.where(lane24 == (r + off) % LANES, x, c)
-                for c, off in zip(cols, (0, 1, LANES - 2, LANES - 1))
-            )
-        return cols
-
     zero24 = jnp.zeros((NV, LANES), F32)
-    c0, c1, c126, c127 = lax.fori_loop(0, ROWS // 4, extract, (zero24,) * 4)
+    cols = (zero24,) * 4
+    for row in range(ROWS):
+        x = roll(row_of(row), row)
+        cols = tuple(
+            jnp.where(lane24 == (row + off) % LANES, x, c)
+            for c, off in zip(cols, (0, 1, LANES - 2, LANES - 1))
+        )
+    c0, c1, c126, c127 = cols
     c1 = roll(c1, -1)
     c126 = roll(c126, 2)
     c127 = roll(c127, 1)
@@ -208,8 +207,8 @@
         [w[0:72], bias8, w[72:144], zeros8, w[144:216], zeros8, zeros8, zeros8], axis=0
     )
     wt[...] = wfull.T.astype(BF16)
-    owp = jnp.concatenate([ow[...].astype(F32) * 0.5, jnp.zeros((256, 104), F32)], axis=1)
-    owt[...] = owp.T[0:32].astype(BF16)
+    owp = ow[...].astype(F32) * 0.5
+    owt[...] = jnp.concatenate([owp, jnp.zeros((8, 256), F32)], axis=0).astype(BF16)
     tail = jnp.zeros((16, LANES), BF16)
     s1[68 * SLAB : 68 * SLAB + 16, :] = tail
     s2[66 * SLAB : 66 * SLAB + 16, :] = tail
@@ -264,20 +263,13 @@
     c127e = own(c127, LANES - 1)
 
     def put1(n, x):
-        s1[pl.ds(pl.multiple_of(n * SLAB, 16), SLAB), :] = slab(
-            x, roll(cm1, (LANES - n) % LANES), roll(cp0, (2 * LANES - 1 - n) % LANES)
-        )
+        s1[n * SLAB : (n + 1) * SLAB, :] = slab(x, roll(cm1, -n), roll(cp0, LANES - 1 - n))
 
     for n, x in ((0, n0), (1, n1), (ROWS + 2, m0), (ROWS + 3, m1)):
         put1(n, x)
 
-    def build(r4, carry):
-        for q in range(4):
-            r = r4 * 4 + q
-            put1(r + 2, row_of(r))
-        return carry
-
-    lax.fori_loop(0, ROWS // 4, build, 0)
+    for row in range(ROWS):
+        put1(row + 2, row_of(row))
 
     weights = wt[...]
     oweights = owt[...]
@@ -306,9 +298,9 @@
         mid1 = s[pl.ds(base + 2 * SLAB, SLAB), :].astype(F32)[NV : 2 * NV]
         return mid0 + c[0:NV, 0:LANES], mid1 + c[0:NV, LANES : 2 * LANES]
 
-    def step1(t3, carry):
-        for q in range(3):
-            n = (t3 * 3 + q) * 2
+    def step1(outer, carry):
+        for q in range(11):
+            n = (outer * 11 + q) * 2
             for d, m in enumerate(tile(s1, n)):
                 at = n + d
                 keep = ((at > 0) | first) & ((at < ROWS + 1) | last)
@@ -320,7 +312,7 @@
                 )
         return carry
 
-    lax.fori_loop(0, 11, step1, 0)
+    lax.fori_loop(0, 3, step1, 0)
 
     flat = oi[0]
     v_of, r_of, c_of = flat // 8192, (flat // LANES) % ROWS, flat % LANES
@@ -336,8 +328,8 @@
         )
 
     def step2(s2i, carry):
-        for q in range(2):
-            t = partner(s2i * 2 + q)
+        for q in range(8):
+            t = partner(s2i * 8 + q)
             f0, f1 = tile(s2, t * 2)
             f = jnp.concatenate([f0, f1], axis=0).astype(BF16)
             fc[t] = f
@@ -350,7 +342,7 @@
             acc[...] += total
         return carry
 
-    lax.fori_loop(0, NE // 2, step2, 0)
+    lax.fori_loop(0, NE // 8, step2, 0)
 
     pick_s[0] = jnp.sum(acc[...], axis=0, keepdims=True)
 
@@ -499,17 +491,17 @@
 
 
 def per_device(x, cw, cb, ow, oi, oc, ov, og):
-    anyspec = pl.BlockSpec(memory_space=pl.ANY)
+    hbm = pl.BlockSpec(memory_space=pltpu.HBM)
     return pl.pallas_call(
         kernel,
         out_shape=jax.ShapeDtypeStruct(x.shape, x.dtype),
-        in_specs=[anyspec] * 8,
+        in_specs=[hbm] * 8,
         out_specs=pl.BlockSpec(memory_space=pltpu.VMEM),
         scratch_shapes=[
             pltpu.VMEM(x.shape, BF16),
             pltpu.VMEM(cw.shape, BF16),
             pltpu.VMEM((1, 256), F32),
-            pltpu.VMEM(ow.shape, BF16),
+            pltpu.VMEM((NV, 256), BF16),
             pltpu.VMEM((1, 1, NOBS), jnp.int32),
             pltpu.VMEM((1, 1), jnp.int32),
             pltpu.VMEM((1, 1, NOBS), F32),
@@ -551,10 +543,10 @@
             pltpu.SemaphoreType.DMA((NE,)),
         ],
         compiler_params=pltpu.CompilerParams(
-            collective_id=0, has_side_effects=True, vmem_limit_bytes=48 * 1024 * 1024
+            collective_id=0, has_side_effects=True, vmem_limit_bytes=67043328
         ),
         name="cycle",
-    )(x, cw, cb.reshape(1, 256), ow, oi, oc, ov, og)
+    )(x, cw, cb.reshape(1, 256), ow.T, oi, oc, ov, og)
 
 
 def solution(mesh):

time: 92.1 us -> 85.7 us (0.931)
  Pallas kernels: 87.6 us -> 83.1 us
  local copies, waits for them, and re-layouts: 3.5 us -> 1.77 us
    pallas_call x1, Pallas kernels: 87.6 us -> 83.1 us  [per_device(): pl.pallas_call(kernel, out_shape=jax.ShapeDtypeStruct(x.shape, x.dtype),...]
    unnamed x14 -> x1, local copies, waits for them, and re-layouts: 3.5 us -> 1.77 us
where the time goes in v2:
time: 85.7 us; the launch traced here: 85.5 us
  Pallas kernels  83.1 us (97%)
  local copies, waits for them, and re-layouts  1.77 us (2%)
    pallas_call x1, Pallas kernels, per_device(): pl.pallas_call(kernel, out_shape=jax.ShapeDtypeStruct(x.shape, x.dtype),...  83.1 us
    unnamed x1, local copies, waits for them, and re-layouts  1.77 us

profile of v2, /device:TPU:1, one launch (start us, length us, event | category | flops | bytes accessed | tf_op | source)
XLA Modules:
  0.0 85.5 jit_solution(6698928464869697385)
XLA Ops:
  0.7 83.1 %cycle.1 = bf16[1,24,64,128]{3,2,1,0:T(8,128)(2,1)} custom-call(bf16[1,24,64,128]{3,2,1,0:T(8,128)(2,1)} %x_hbm.1, bf16[216,256]{1,0:T(8,128)(2,1)} %cw_hbm.1, f32[1,256]{1,0:T(1,128)} %bitcast.3, bf16[24,256]{1,0:T(8,128)(2,1)} %bitcast.2, s32[1,1,256]{2,1,0:T(1,128)} %oi_hbm.1, s32[1,1]{1,0:T(1,128)S(6)} %copy.10.oc_hbm, f32[1,1,256]{2,1,0:T(1,128)} %ov_hbm.1, ...), custom_call_target="tpu_custom_call" | custom-call | tf_op jit(solution)/shard_map/cycle/pallas_call | solution.py:495
  83.8 1.8 %copy.11 = bf16[1,24,64,128]{3,2,1,0:T(8,128)(2,1)} copy(bf16[1,24,64,128]{3,2,1,0:T(8,128)(2,1)} %cycle.1) | data formatting | bytes 786432

commit v3 on v2

--- a/solution.py
+++ b/solution.py
@@ -68,58 +68,43 @@
     return dot(ow, gelu2(pre))
 
 
-def kernel(
-    x_hbm, cw_hbm, cb_hbm, ow_hbm, oi_hbm, oc_hbm, ov_hbm, og_hbm, out_ref,
-    xv, cw, cb, ow, oi, oc, ov, og,
-    big, s1, s2, wt, owt, hrow_s, hcol_s, hrow, hcol, obs_s, obs_r,
-    fc, recv, back, res, pick_s, hx, gsend, grecv, acc, ep, oh, sp, ets,
-    load_sem, hsend, hrecv, asend, arecv, psend, precv, gsend_sem, grecv_sem,
-    bsend, brecv,
-):
+def fill(big, xv):
+    for v in range(NV):
+        big[v * PITCH : v * PITCH + ROWS, :] = xv[0, v].astype(F32)
+
+
+def place():
     k = lax.axis_index("ens")
     i = lax.axis_index("lat")
     j = lax.axis_index("lon")
-    i2 = (i + 2) % NA
-    k_hi, k_y, k_c = k // 16, (k // 2) % 8, k % 2
 
     def peer(dk, di, dj):
         return ((k + dk) % NE, (i + di) % NA, (j + dj) % NB)
 
-    def partner(s):
-        u = s // 4
-        dy = ((u + 1) // 2) * (2 * (u % 2) - 1)
-        hi = (k_hi + s) % 2
-        y = (k_y + 8 + dy) % 8
-        c = (k_c + s // 2) % 2
-        return hi * 16 + y * 2 + c
-
-    loads = [
-        pltpu.make_async_copy(src, dst, load_sem.at[n])
-        for n, (src, dst) in enumerate(
-            [(x_hbm, xv), (cw_hbm, cw), (cb_hbm, cb), (ow_hbm, ow),
-             (oi_hbm, oi), (oc_hbm, oc), (ov_hbm, ov), (og_hbm, og)]
-        )
-    ]
-    for c in loads:
-        c.start()
-
+    return k, i, j, peer
+
+
+def meet(peers):
     barrier = pltpu.get_barrier_semaphore()
-    for di in range(NA):
-        for dj in range(NB):
-            if di or dj:
-                pl.semaphore_signal(
-                    barrier, inc=1, device_id=peer(0, di, dj), device_id_type=MESH
-                )
-    for dk in range(1, NE):
-        pl.semaphore_signal(barrier, inc=1, device_id=peer(dk, 2, 0), device_id_type=MESH)
-
-    for c in loads:
-        c.wait()
-
+    for to in peers:
+        pl.semaphore_signal(barrier, inc=1, device_id=to, device_id_type=MESH)
+    return lambda: pl.semaphore_wait(barrier, len(peers))
+
+
+def halo_kernel(
+    x_hbm, oc, ov, og, hcol_s, hrow, hcol, obs_r,
+    xv, big, hrow_s, obs_s, load_sem, hsend, hrecv,
+):
+    k, i, j, peer = place()
+    load = pltpu.make_async_copy(x_hbm, xv, load_sem)
+    load.start()
+    met = meet(
+        [peer(0, di, dj) for di in (0, 1, -1) for dj in (0, 1, -1) if di or dj] + [peer(0, 2, 0)]
+    )
+    load.wait()
     lane24 = lane_iota((NV, LANES))
 
-    for v in range(NV):
-        big[v * PITCH : v * PITCH + ROWS, :] = xv[0, v].astype(F32)
+    fill(big, xv)
 
     def row_of(r):
         return big[pl.ds(r, NV, stride=PITCH), :]
@@ -145,7 +130,7 @@
     obs_s[1:2, :] = og[0] * live
     obs_s[2:8, :] = jnp.zeros((6, NOBS), F32)
 
-    pl.semaphore_wait(barrier, NA * NB - 1 + NE - 1)
+    met()
 
     def halo(src, dst, n, di, dj):
         return pltpu.make_async_remote_copy(
@@ -194,6 +179,56 @@
         hrow[1] = jnp.zeros((2 * NV, LANES), BF16)
         hcol[4] = jnp.zeros((2 * NV, LANES), BF16)
         hcol[5] = jnp.zeros((2 * NV, LANES), BF16)
+
+    for c in sides:
+        c.wait()
+    obs_copy.wait()
+
+    @pl.when(i > 0)
+    def _():
+        for c in north:
+            c.wait_recv()
+
+    @pl.when(i < NA - 1)
+    def _():
+        for c in north:
+            c.wait_send()
+        for c in south:
+            c.wait_recv()
+
+    @pl.when(i > 0)
+    def _():
+        for c in south:
+            c.wait_send()
+
+
+def kernel(
+    xv, cw, cb, ow, oi, hcol_s, hrow, hcol, obs_r, out_ref,
+    big, s1, s2, wt, owt,
+    fc, recv, back, res, pick_s, hx, gsend, grecv, ep, oh, sp, ets,
+    asend, arecv, psend, precv, gsend_sem, grecv_sem, bsend, brecv,
+):
+    k, i, j, peer = place()
+    i2 = (i + 2) % NA
+    k_hi, k_y, k_c = k // 16, (k // 2) % 8, k % 2
+
+    def partner(s):
+        u = s // 4
+        dy = ((u + 1) // 2) * (2 * (u % 2) - 1)
+        hi = (k_hi + s) % 2
+        y = (k_y + 8 + dy) % 8
+        c = (k_c + s // 2) % 2
+        return hi * 16 + y * 2 + c
+
+    met = meet(
+        [peer(0, di, dj) for di in range(NA) for dj in range(NB) if di or dj]
+        + [peer(dk, 2, 0) for dk in range(1, NE)]
+    )
+    lane24 = lane_iota((NV, LANES))
+    fill(big, xv)
+
+    def row_of(r):
+        return big[pl.ds(r, NV, stride=PITCH), :]
 
     w = cw[...].astype(F32)
     b = cb[...]
@@ -213,27 +248,6 @@
     s1[68 * SLAB : 68 * SLAB + 16, :] = tail
     s2[66 * SLAB : 66 * SLAB + 16, :] = tail
 
-    for c in sides:
-        c.wait()
-    obs_copy.wait()
-
-    @pl.when(i > 0)
-    def _():
-        for c in north:
-            c.wait_recv()
-
-    @pl.when(i < NA - 1)
-    def _():
-        for c in north:
-            c.wait_send()
-        for c in south:
-            c.wait_recv()
-
-    @pl.when(i > 0)
-    def _():
-        for c in south:
-            c.wait_send()
-
     def pair(ref, n):
         both = ref[n].astype(F32)
         return both[0:NV], both[NV : 2 * NV]
@@ -259,8 +273,8 @@
             out = jnp.where(lane24 == at, roll(x, at - lane), out)
         return out
 
-    c0e = own(c0, 0)
-    c127e = own(c127, LANES - 1)
+    c0e = own(pair(hcol_s, 0)[0], 0)
+    c127e = own(pair(hcol_s, 1)[1], LANES - 1)
 
     def put1(n, x):
         s1[n * SLAB : (n + 1) * SLAB, :] = slab(x, roll(cm1, -n), roll(cp0, LANES - 1 - n))
@@ -316,9 +330,33 @@
 
     flat = oi[0]
     v_of, r_of, c_of = flat // 8192, (flat // LANES) % ROWS, flat % LANES
-    where_row = r_of * NV + v_of
     oh[...] = marks(row_iota((LANES, NOBS)) == c_of)
-    acc[...] = jnp.zeros((8, NOBS), F32)
+
+    def gather(outer, taps):
+        base = pl.multiple_of(outer * (6 * SLAB), 16)
+        at_c = dot(s2[pl.ds(base, 6 * SLAB), :], oh[...]).astype(BF16)
+        for q in range(6):
+            part = at_c[q * SLAB : (q + 1) * SLAB]
+            n = outer * 6 + q
+            taps = tuple(t + part * marks(r_of == n - a) for a, t in enumerate(taps))
+        return taps
+
+    taps = lax.fori_loop(0, 11, gather, (jnp.zeros((SLAB, NOBS), BF16),) * 3)
+    for a in range(3):
+        ep[a * SLAB : (a + 1) * SLAB, :] = taps[a]
+    ep[3 * SLAB : 256, :] = jnp.zeros((16, NOBS), BF16)
+    seen = taps[1].astype(F32)[NV : 2 * NV] + changes(weights, oweights, ep[...])[0:NV]
+    seen = seen.astype(BF16).astype(F32)
+    pick_s[0] = jnp.sum(jnp.where(row_iota((NV, NOBS)) == v_of, seen, 0.0), axis=0, keepdims=True)
+
+    def send_pick(t):
+        return pltpu.make_async_remote_copy(
+            src_ref=pick_s.at[0], dst_ref=hx.at[k], send_sem=psend.at[t], recv_sem=precv.at[k],
+            device_id=(t, i2, j), device_id_type=MESH,
+        )
+
+    def over(n, body):
+        lax.fori_loop(0, n, lambda s, c: (body(s), c)[1], 0)
 
     def send_tile(s):
         t = partner(s)
@@ -327,36 +365,20 @@
             device_id=(t, i2, j), device_id_type=MESH,
         )
 
-    def step2(s2i, carry):
+    def step2(outer, carry):
         for q in range(8):
-            t = partner(s2i * 8 + q)
+            s = outer * 8 + q
+            t = partner(s)
             f0, f1 = tile(s2, t * 2)
-            f = jnp.concatenate([f0, f1], axis=0).astype(BF16)
-            fc[t] = f
-            at_c = dot(f, oh[...])
-            hit = row_iota((2 * NV, NOBS)) + t * (2 * NV) == where_row
-            sel = jnp.where(hit, at_c, 0.0)
-            total = sel[0:8]
-            for g in range(1, 6):
-                total = total + sel[8 * g : 8 * g + 8]
-            acc[...] += total
+            fc[t] = jnp.concatenate([f0, f1], axis=0).astype(BF16)
+            if q:
+                send_tile(s - 1).start()
+        send_tile(outer * 8 + 7).start()
         return carry
 
-    lax.fori_loop(0, NE // 8, step2, 0)
-
-    pick_s[0] = jnp.sum(acc[...], axis=0, keepdims=True)
-
-    def send_pick(t):
-        return pltpu.make_async_remote_copy(
-            src_ref=pick_s.at[0], dst_ref=hx.at[k], send_sem=psend.at[t], recv_sem=precv.at[k],
-            device_id=(t, i2, j), device_id_type=MESH,
-        )
-
-    def over(n, body):
-        lax.fori_loop(0, n, lambda s, c: (body(s), c)[1], 0)
-
+    met()
     over(NE, lambda s: send_pick(partner(s)).start())
-    over(NE, lambda s: send_tile(s).start())
+    lax.fori_loop(0, 2, step2, 0)
 
     def recv_pick(t):
         return pltpu.make_async_remote_copy(
@@ -402,6 +424,7 @@
     others = [(di, dj) for di in range(NA) for dj in range(NB) if di or dj]
     for di, dj in others:
         send_gram(di, dj).start()
+    lax.fori_loop(2, 4, step2, 0)
     for di, dj in others:
         recv_gram(di, dj).wait_recv()
 
@@ -491,32 +514,43 @@
 
 
 def per_device(x, cw, cb, ow, oi, oc, ov, og):
-    hbm = pl.BlockSpec(memory_space=pltpu.HBM)
+    vmem = pl.BlockSpec(memory_space=pltpu.VMEM)
+    hcol_s, hrow, hcol, obs_r = pl.pallas_call(
+        halo_kernel,
+        out_shape=(
+            jax.ShapeDtypeStruct((2, 2 * NV, LANES), BF16),
+            jax.ShapeDtypeStruct((2, 2 * NV, LANES), BF16),
+            jax.ShapeDtypeStruct((6, 2 * NV, LANES), BF16),
+            jax.ShapeDtypeStruct((8, NOBS), F32),
+        ),
+        in_specs=[pl.BlockSpec(memory_space=pl.ANY), vmem, vmem, vmem],
+        out_specs=(vmem,) * 4,
+        scratch_shapes=[
+            pltpu.VMEM(x.shape, BF16),
+            pltpu.VMEM((NV * PITCH, LANES), F32),
+            pltpu.VMEM((2, 2 * NV, LANES), BF16),
+            pltpu.VMEM((8, NOBS), F32),
+            pltpu.SemaphoreType.DMA,
+            pltpu.SemaphoreType.DMA((9,)),
+            pltpu.SemaphoreType.DMA((9,)),
+        ],
+        compiler_params=pltpu.CompilerParams(
+            collective_id=0, has_side_effects=True, vmem_limit_bytes=16 * 1024 * 1024
+        ),
+        cost_estimate=pl.CostEstimate(flops=10**10, bytes_accessed=10**6, transcendentals=0),
+        name="halo",
+    )(x, oc, ov, og)
     return pl.pallas_call(
         kernel,
         out_shape=jax.ShapeDtypeStruct(x.shape, x.dtype),
-        in_specs=[hbm] * 8,
-        out_specs=pl.BlockSpec(memory_space=pltpu.VMEM),
+        in_specs=[vmem] * 9,
+        out_specs=vmem,
         scratch_shapes=[
-            pltpu.VMEM(x.shape, BF16),
-            pltpu.VMEM(cw.shape, BF16),
-            pltpu.VMEM((1, 256), F32),
-            pltpu.VMEM((NV, 256), BF16),
-            pltpu.VMEM((1, 1, NOBS), jnp.int32),
-            pltpu.VMEM((1, 1), jnp.int32),
-            pltpu.VMEM((1, 1, NOBS), F32),
-            pltpu.VMEM((1, 1, NOBS), F32),
             pltpu.VMEM((NV * PITCH, LANES), F32),
             pltpu.VMEM((68 * SLAB + 16, LANES), BF16),
             pltpu.VMEM((66 * SLAB + 16, LANES), BF16),
             pltpu.VMEM((256, 256), BF16),
             pltpu.VMEM((32, 256), BF16),
-            pltpu.VMEM((2, 2 * NV, LANES), BF16),
-            pltpu.VMEM((2, 2 * NV, LANES), BF16),
-            pltpu.VMEM((2, 2 * NV, LANES), BF16),
-            pltpu.VMEM((6, 2 * NV, LANES), BF16),
-            pltpu.VMEM((8, NOBS), F32),
-            pltpu.VMEM((8, NOBS), F32),
             pltpu.VMEM((NE, 2 * NV, LANES), BF16),
             pltpu.VMEM((NE, 2 * NV, LANES), BF16),
             pltpu.VMEM((NE, 2 * NV, LANES), BF16),
@@ -525,14 +559,10 @@
             pltpu.VMEM((NE, 1, NOBS), F32),
             pltpu.VMEM((16, LANES), F32),
             pltpu.VMEM((NA * NB, 16, LANES), F32),
-            pltpu.VMEM((8, NOBS), F32),
             pltpu.VMEM((256, 256), BF16),
             pltpu.VMEM((LANES, NOBS), BF16),
             pltpu.VMEM((NE, 512), BF16),
             pltpu.VMEM((2, NE, NE), BF16),
-            pltpu.SemaphoreType.DMA((8,)),
-            pltpu.SemaphoreType.DMA((9,)),
-            pltpu.SemaphoreType.DMA((9,)),
             pltpu.SemaphoreType.DMA((NE,)),
             pltpu.SemaphoreType.DMA((NE,)),
             pltpu.SemaphoreType.DMA((NE,)),
@@ -543,10 +573,10 @@
             pltpu.SemaphoreType.DMA((NE,)),
         ],
         compiler_params=pltpu.CompilerParams(
-            collective_id=0, has_side_effects=True, vmem_limit_bytes=67043328
+            collective_id=1, has_side_effects=True, vmem_limit_bytes=32 * 1024 * 1024
         ),
         name="cycle",
-    )(x, cw, cb.reshape(1, 256), ow.T, oi, oc, ov, og)
+    )(x, cw, cb.reshape(1, 256), ow.T, oi, hcol_s, hrow, hcol, obs_r)
 
 
 def solution(mesh):

time: 85.7 us -> 76 us (0.89)
  Pallas kernels: 83.1 us -> 72 us
  local copies, waits for them, and re-layouts: 1.77 us -> 3.07 us
    pallas_call x1, Pallas kernels: 83.1 us -> 60.2 us  [per_device(): pl.pallas_call(kernel, out_shape=jax.ShapeDtypeStruct(x.shape, x.dtype),...]
    pallas_call x0 -> x1, Pallas kernels: none -> 11.8 us  [per_device(): pl.pallas_call(halo_kernel, out_shape=(jax.ShapeDtypeStruct((2, 2 * NV, L...]
    unnamed x1 -> x17, local copies, waits for them, and re-layouts: 1.77 us -> 3.07 us
where the time goes in v3:
time: 76 us; the launch traced here: 75.8 us
  Pallas kernels  72 us (95%)
  local copies, waits for them, and re-layouts  3.07 us (4%)
    pallas_call x1, Pallas kernels, per_device(): pl.pallas_call(kernel, out_shape=jax.ShapeDtypeStruct(x.shape, x.dtype),...  60.2 us
    pallas_call x1, Pallas kernels, per_device(): pl.pallas_call(halo_kernel, out_shape=(jax.ShapeDtypeStruct((2, 2 * NV, L...  11.8 us
    unnamed x17, local copies, waits for them, and re-layouts  3.07 us

profile of v3, /device:TPU:1, one launch (start us, length us, event | category | flops | bytes accessed | tf_op | source)
XLA Modules:
  0.0 75.8 jit_solution(12377321879952182445)
XLA Ops:
  0.7 0.0 copy-start.7
  0.7 0.0 copy-start.6
  0.7 0.7 copy-done.7
  1.3 0.0 copy-done.6
  1.3 0.0 copy-start
  1.4 1.0 %copy-done = bf16[1,24,64,128]{3,2,1,0:T(8,128)(2,1)S(1)} copy-done((bf16[1,24,64,128]{3,2,1,0:T(8,128)(2,1)S(1)}, bf16[1,24,64,128]{3,2,1,0:T(8,128)(2,1)}, u32[]{:S(2)}) %copy-start) | copy-done | bytes 393240
  2.3 0.0 copy-start.1
  2.3 0.0 copy-start.2
  2.3 0.0 copy-start.3
  2.4 0.0 copy-start.5
  2.4 11.8 %halo.1 = (bf16[2,48,128]{2,1,0:T(8,128)(2,1)S(1)}, bf16[2,48,128]{2,1,0:T(8,128)(2,1)S(1)}, bf16[6,48,128]{2,1,0:T(8,128)(2,1)S(1)}, f32[8,256]{1,0:T(8,128)S(1)}) custom-call(bf16[1,24,64,128]{3,2,1,0:T(8,128)(2,1)S(1)} %copy-done, s32[1,1]{1,0:T(1,128)S(6)} %copy.10.oc, f32[1,1,256]{2,1,0:T(1,128)S(1)} %copy-done.6, f32[1,1,256]{2,1,0:T(1,128)S(1)} %copy-done.7), custom_call_target="tpu_custom_call" | custom-call | flops 10000000000 | bytes 1000000 | tf_op jit(solution)/shard_map/halo/pallas_call | solution.py:518
  14.2 0.0 copy-start.4
  14.2 0.0 copy-done.1
  14.2 0.0 copy-done.2
  14.2 0.0 copy-done.3
  14.2 0.0 copy-done.5
  14.2 0.6 copy-done.4
  14.8 60.2 %cycle.1 = bf16[1,24,64,128]{3,2,1,0:T(8,128)(2,1)S(1)} custom-call(bf16[1,24,64,128]{3,2,1,0:T(8,128)(2,1)S(1)} %copy-done.1, bf16[216,256]{1,0:T(8,128)(2,1)S(1)} %copy-done.2, f32[1,256]{1,0:T(1,128)S(1)} %bitcast.3, bf16[24,256]{1,0:T(8,128)(2,1)S(1)} %bitcast.2, s32[1,1,256]{2,1,0:T(1,128)S(1)} %copy-done.5, ...), custom_call_target="tpu_custom_call" | custom-call | tf_op jit(solution)/shard_map/cycle/pallas_call | solution.py:543
  75.1 0.7 copy.11
Async XLA Ops:
  0.7 0.7 copy-start.7
  0.7 0.7 copy-start.6
  1.3 1.0 %copy-start = (bf16[1,24,64,128]{3,2,1,0:T(8,128)(2,1)S(1)}, bf16[1,24,64,128]{3,2,1,0:T(8,128)(2,1)}, u32[]{:S(2)}) copy-start(bf16[1,24,64,128]{3,2,1,0:T(8,128)(2,1)} %xv.1) | copy-start | bytes 1179652
  2.3 11.8 %copy-start.1 = (bf16[1,24,64,128]{3,2,1,0:T(8,128)(2,1)S(1)}, bf16[1,24,64,128]{3,2,1,0:T(8,128)(2,1)}, u32[]{:S(2)}) copy-start(bf16[1,24,64,128]{3,2,1,0:T(8,128)(2,1)} %xv.1) | copy-start | bytes 1179652
  2.3 11.8 %copy-start.2 = (bf16[216,256]{1,0:T(8,128)(2,1)S(1)}, bf16[216,256]{1,0:T(8,128)(2,1)}, u32[]{:S(2)}) copy-start(bf16[216,256]{1,0:T(8,128)(2,1)} %cw.1) | copy-start | bytes 331780
  2.3 11.8 %copy-start.3 = (bf16[256,24]{0,1:T(8,128)(2,1)S(1)}, bf16[256,24]{0,1:T(8,128)(2,1)}, u32[]{:S(2)}) copy-start(bf16[256,24]{0,1:T(8,128)(2,1)} %param.11) | copy-start | bytes 36868
  2.4 11.9 %copy-start.5 = (s32[1,1,256]{2,1,0:T(1,128)S(1)}, s32[1,1,256]{2,1,0:T(1,128)}, u32[]{:S(2)}) copy-start(s32[1,1,256]{2,1,0:T(1,128)} %oi.1) | copy-start | bytes 3076
  14.2 0.7 copy-start.4

commit v4 on v3

--- a/solution.py
+++ b/solution.py
@@ -92,14 +92,14 @@
 
 
 def halo_kernel(
-    x_hbm, oc, ov, og, hcol_s, hrow, hcol, obs_r,
-    xv, big, hrow_s, obs_s, load_sem, hsend, hrecv,
+    x_hbm, hcol_s, hrow, hcol,
+    xv, big, hrow_s, load_sem, hsend, hrecv,
 ):
     k, i, j, peer = place()
     load = pltpu.make_async_copy(x_hbm, xv, load_sem)
     load.start()
     met = meet(
-        [peer(0, di, dj) for di in (0, 1, -1) for dj in (0, 1, -1) if di or dj] + [peer(0, 2, 0)]
+        [peer(0, di, dj) for di in (0, 1, -1) for dj in (0, 1, -1) if di or dj]
     )
     load.wait()
     lane24 = lane_iota((NV, LANES))
@@ -125,11 +125,6 @@
     hcol_s[1] = jnp.concatenate([c126, c127], axis=0).astype(BF16)
     hrow_s[0] = jnp.concatenate([row_of(0), row_of(1)], axis=0).astype(BF16)
     hrow_s[1] = jnp.concatenate([row_of(ROWS - 2), row_of(ROWS - 1)], axis=0).astype(BF16)
-    live = (lane_iota((1, NOBS)) < oc[...]).astype(F32)
-    obs_s[0:1, :] = ov[0]
-    obs_s[1:2, :] = og[0] * live
-    obs_s[2:8, :] = jnp.zeros((6, NOBS), F32)
-
     met()
 
     def halo(src, dst, n, di, dj):
@@ -152,7 +147,6 @@
         halo(hcol_s.at[1], hcol.at[0], 2, 0, 1),
         halo(hcol_s.at[0], hcol.at[1], 3, 0, -1),
     ]
-    obs_copy = halo(obs_s, obs_r, 8, 2, 0)
 
     @pl.when(i < NA - 1)
     def _():
@@ -166,7 +160,6 @@
 
     for c in sides:
         c.start()
-    obs_copy.start()
 
     @pl.when(i == 0)
     def _():
@@ -182,7 +175,6 @@
 
     for c in sides:
         c.wait()
-    obs_copy.wait()
 
     @pl.when(i > 0)
     def _():
@@ -203,16 +195,17 @@
 
 
 def kernel(
-    xv, cw, cb, ow, oi, hcol_s, hrow, hcol, obs_r, out_ref,
+    xv, cw, cb, ow, oi, oc, ov, og, hcol_s, hrow, hcol, out_ref,
     big, s1, s2, wt, owt,
-    fc, recv, back, res, pick_s, hx, gsend, grecv, ep, oh, sp, ets,
-    asend, arecv, psend, precv, gsend_sem, grecv_sem, bsend, brecv,
+    fc, recv, back, res, pick_s, hx, gsend, grecv, ep, oh, sp, ets, hs, kr, fr, ob, obs_s, obs_r,
+    asend, arecv, psend, precv, gsend_sem, grecv_sem, bsend, brecv, osem,
 ):
     k, i, j, peer = place()
     i2 = (i + 2) % NA
     k_hi, k_y, k_c = k // 16, (k // 2) % 8, k % 2
 
     def partner(s):
+        s = (s + 1) % NE
         u = s // 4
         dy = ((u + 1) // 2) * (2 * (u % 2) - 1)
         hi = (k_hi + s) % 2
@@ -222,13 +215,16 @@
 
     met = meet(
         [peer(0, di, dj) for di in range(NA) for dj in range(NB) if di or dj]
-        + [peer(dk, 2, 0) for dk in range(1, NE)]
+        + [peer(dk, di, 0) for dk in range(1, NE) for di in (0, 2)]
     )
     lane24 = lane_iota((NV, LANES))
     fill(big, xv)
 
     def row_of(r):
         return big[pl.ds(r, NV, stride=PITCH), :]
+
+    def over(n, body):
+        lax.fori_loop(0, n, lambda s, c: (body(s), c)[1], 0)
 
     w = cw[...].astype(F32)
     b = cb[...]
@@ -304,18 +300,24 @@
     mw = jnp.where(inside, roll(cm1, -1) + ch[0:NV, 0:LANES], 0.0)
     me = jnp.where(inside, roll(cp0, -1) + ch[0:NV, LANES : 2 * LANES], 0.0)
 
-    def tile(s, n):
+    def hide(s, n, q):
         base = pl.multiple_of(n * SLAB, 16)
         p = jnp.concatenate([s[pl.ds(base, 256), :], s[pl.ds(base + SLAB, 256), :]], axis=1)
-        c = changes(weights, oweights, p)
+        hs[q] = gelu2(dot(wt[...], p))
+
+    def tile(s, n, q):
+        base = pl.multiple_of(n * SLAB, 16)
+        c = dot(owt[...], hs[q])
         mid0 = s[pl.ds(base + SLAB, SLAB), :].astype(F32)[NV : 2 * NV]
         mid1 = s[pl.ds(base + 2 * SLAB, SLAB), :].astype(F32)[NV : 2 * NV]
         return mid0 + c[0:NV, 0:LANES], mid1 + c[0:NV, LANES : 2 * LANES]
 
     def step1(outer, carry):
         for q in range(11):
+            hide(s1, (outer * 11 + q) * 2, q)
+        for q in range(11):
             n = (outer * 11 + q) * 2
-            for d, m in enumerate(tile(s1, n)):
+            for d, m in enumerate(tile(s1, n, q)):
                 at = n + d
                 keep = ((at > 0) | first) & ((at < ROWS + 1) | last)
                 m = jnp.where(keep, m, 0.0)
@@ -328,20 +330,29 @@
 
     lax.fori_loop(0, 3, step1, 0)
 
+    live = (lane_iota((1, NOBS)) < oc[...]).astype(F32)
+    obs_s[0:1, :] = ov[0]
+    obs_s[1:2, :] = og[0] * live
+    obs_s[2:8, :] = jnp.zeros((6, NOBS), F32)
+
     flat = oi[0]
     v_of, r_of, c_of = flat // 8192, (flat // LANES) % ROWS, flat % LANES
     oh[...] = marks(row_iota((LANES, NOBS)) == c_of)
 
+    def columns(outer):
+        rows = pl.ds(pl.multiple_of(outer * (22 * SLAB), 16), 22 * SLAB)
+        ob[rows, :] = dot(s2[rows, :], oh[...]).astype(BF16)
+
+    over(3, columns)
+
     def gather(outer, taps):
-        base = pl.multiple_of(outer * (6 * SLAB), 16)
-        at_c = dot(s2[pl.ds(base, 6 * SLAB), :], oh[...]).astype(BF16)
-        for q in range(6):
-            part = at_c[q * SLAB : (q + 1) * SLAB]
-            n = outer * 6 + q
+        for q in range(11):
+            n = outer * 11 + q
+            part = ob[pl.ds(pl.multiple_of(n * SLAB, 16), SLAB), :]
             taps = tuple(t + part * marks(r_of == n - a) for a, t in enumerate(taps))
         return taps
 
-    taps = lax.fori_loop(0, 11, gather, (jnp.zeros((SLAB, NOBS), BF16),) * 3)
+    taps = lax.fori_loop(0, 6, gather, (jnp.zeros((SLAB, NOBS), BF16),) * 3)
     for a in range(3):
         ep[a * SLAB : (a + 1) * SLAB, :] = taps[a]
     ep[3 * SLAB : 256, :] = jnp.zeros((16, NOBS), BF16)
@@ -355,29 +366,37 @@
             device_id=(t, i2, j), device_id_type=MESH,
         )
 
-    def over(n, body):
-        lax.fori_loop(0, n, lambda s, c: (body(s), c)[1], 0)
-
     def send_tile(s):
         t = partner(s)
         return pltpu.make_async_remote_copy(
             src_ref=fc.at[t], dst_ref=recv.at[k], send_sem=asend.at[t], recv_sem=arecv.at[k],
-            device_id=(t, i2, j), device_id_type=MESH,
+            device_id=(t, i, j), device_id_type=MESH,
         )
 
     def step2(outer, carry):
+        for q in range(8):
+            hide(s2, partner(outer * 8 + q) * 2, q)
         for q in range(8):
             s = outer * 8 + q
             t = partner(s)
-            f0, f1 = tile(s2, t * 2)
+            f0, f1 = tile(s2, t * 2, q)
             fc[t] = jnp.concatenate([f0, f1], axis=0).astype(BF16)
             if q:
                 send_tile(s - 1).start()
-        send_tile(outer * 8 + 7).start()
+
+        @pl.when(outer < 3)
+        def _():
+            send_tile(outer * 8 + 7).start()
+
         return carry
 
+    obs_copy = pltpu.make_async_remote_copy(
+        src_ref=obs_s, dst_ref=obs_r, send_sem=osem.at[0], recv_sem=osem.at[1],
+        device_id=(k, i2, j), device_id_type=MESH,
+    )
     met()
     over(NE, lambda s: send_pick(partner(s)).start())
+    obs_copy.start()
     lax.fori_loop(0, 2, step2, 0)
 
     def recv_pick(t):
@@ -389,6 +408,7 @@
     over(NE, lambda t: recv_pick(t).wait_recv())
 
     values = hx[:, 0, :]
+    obs_copy.wait()
     value = obs_r[0:1, :]
     weight = obs_r[1:2, :]
     mean = jnp.mean(values, axis=0, keepdims=True)
@@ -467,39 +487,59 @@
         a = dot(spread, e).astype(BF16)
         return jnp.where(same, dot(a, sp[...]), 0.0).astype(BF16)
 
-    kr_hi = kron(ets[0])
-    kr_lo = kron(ets[1])
+    kr[0] = kron(ets[0])
+    kr[1] = kron(ets[1])
 
     def recv_tile(t):
         return pltpu.make_async_remote_copy(
             src_ref=fc.at[t], dst_ref=recv.at[t], send_sem=asend.at[t], recv_sem=arecv.at[t],
-            device_id=(t, i2, j), device_id_type=MESH,
-        )
-
-    over(NE, lambda t: recv_tile(t).wait_recv())
+            device_id=(t, i, j), device_id_type=MESH,
+        )
+
+    recv[k] = fc[k]
+    over(NE - 1, lambda s: recv_tile(partner(s)).wait_recv())
 
     for q in range(3):
-        f = recv[:, 16 * q : 16 * q + 16, :].reshape(512, LANES)
-        o = dot(kr_hi, f) + dot(kr_lo, f)
-        back[:, 16 * q : 16 * q + 16, :] = o.astype(BF16).reshape(NE, 16, LANES)
-
-    def send_back(s):
+        fr[:, q * LANES : (q + 1) * LANES] = recv[:, 16 * q : 16 * q + 16, :].reshape(512, LANES)
+
+    def send_back(t):
+        return pltpu.make_async_remote_copy(
+            src_ref=back.at[t], dst_ref=res.at[k], send_sem=bsend.at[t], recv_sem=brecv.at[k],
+            device_id=(t, i, j), device_id_type=MESH,
+        )
+
+    def recv_back(t):
+        return pltpu.make_async_remote_copy(
+            src_ref=back.at[t], dst_ref=res.at[t], send_sem=bsend.at[t], recv_sem=brecv.at[t],
+            device_id=(t, i, j), device_id_type=MESH,
+        )
+
+    def group(g):
+        return (k // 8 + 1 + g) % 4
+
+    def send_group(g):
+        for e in range(8 if g < 3 else 7):
+            send_back(group(g) * 8 + (k + 1 + e) % 8).start()
+
+    for g in range(4):
+        rows = pl.ds(pl.multiple_of(group(g) * LANES, LANES), LANES)
+        o = (dot(kr[0, rows, :], fr[...]) + dot(kr[1, rows, :], fr[...])).astype(BF16)
+        for q in range(3):
+            back[pl.ds(group(g) * 8, 8), 16 * q : 16 * q + 16, :] = o[
+                :, q * LANES : (q + 1) * LANES
+            ].reshape(8, 16, LANES)
+        if g:
+            send_group(g - 1)
+    send_group(3)
+    res[k] = back[k]
+
+    def finish(s):
         t = partner(s)
-        return pltpu.make_async_remote_copy(
-            src_ref=back.at[t], dst_ref=res.at[k], send_sem=bsend.at[t], recv_sem=brecv.at[k],
-            device_id=(t, i2, j), device_id_type=MESH,
-        )
-
-    def recv_back(t):
-        return pltpu.make_async_remote_copy(
-            src_ref=back.at[t], dst_ref=res.at[t], send_sem=bsend.at[t], recv_sem=brecv.at[t],
-            device_id=(t, i2, j), device_id_type=MESH,
-        )
-
-    over(NE, lambda s: send_back(s).start())
-
-    def finish(t):
-        recv_back(t).wait_recv()
+
+        @pl.when(s < NE - 1)
+        def _():
+            recv_back(t).wait_recv()
+
         big[pl.ds(pl.multiple_of(t * 48, 16), 48), :] = res[t].astype(F32)
 
     over(NE, finish)
@@ -507,29 +547,27 @@
         out_ref[0, v] = big[pl.ds(v, ROWS, stride=NV), :].astype(BF16)
 
     over(NE, lambda t: recv_pick(t).wait_send())
-    over(NE, lambda t: recv_tile(t).wait_send())
-    over(NE, lambda t: recv_back(t).wait_send())
+    over(NE - 1, lambda s: recv_tile(partner(s)).wait_send())
+    over(NE - 1, lambda s: recv_back(partner(s)).wait_send())
     for di, dj in others:
         send_gram(di, dj).wait_send()
 
 
 def per_device(x, cw, cb, ow, oi, oc, ov, og):
     vmem = pl.BlockSpec(memory_space=pltpu.VMEM)
-    hcol_s, hrow, hcol, obs_r = pl.pallas_call(
+    hcol_s, hrow, hcol = pl.pallas_call(
         halo_kernel,
         out_shape=(
             jax.ShapeDtypeStruct((2, 2 * NV, LANES), BF16),
             jax.ShapeDtypeStruct((2, 2 * NV, LANES), BF16),
             jax.ShapeDtypeStruct((6, 2 * NV, LANES), BF16),
-            jax.ShapeDtypeStruct((8, NOBS), F32),
         ),
-        in_specs=[pl.BlockSpec(memory_space=pl.ANY), vmem, vmem, vmem],
-        out_specs=(vmem,) * 4,
+        in_specs=[pl.BlockSpec(memory_space=pl.ANY)],
+        out_specs=(vmem,) * 3,
         scratch_shapes=[
             pltpu.VMEM(x.shape, BF16),
             pltpu.VMEM((NV * PITCH, LANES), F32),
             pltpu.VMEM((2, 2 * NV, LANES), BF16),
-            pltpu.VMEM((8, NOBS), F32),
             pltpu.SemaphoreType.DMA,
             pltpu.SemaphoreType.DMA((9,)),
             pltpu.SemaphoreType.DMA((9,)),
@@ -539,11 +577,11 @@
         ),
         cost_estimate=pl.CostEstimate(flops=10**10, bytes_accessed=10**6, transcendentals=0),
         name="halo",
-    )(x, oc, ov, og)
+    )(x)
     return pl.pallas_call(
         kernel,
         out_shape=jax.ShapeDtypeStruct(x.shape, x.dtype),
-        in_specs=[vmem] * 9,
+        in_specs=[vmem] * 11,
         out_specs=vmem,
         scratch_shapes=[
             pltpu.VMEM((NV * PITCH, LANES), F32),
@@ -563,6 +601,12 @@
             pltpu.VMEM((LANES, NOBS), BF16),
             pltpu.VMEM((NE, 512), BF16),
             pltpu.VMEM((2, NE, NE), BF16),
+            pltpu.VMEM((11, 256, 256), BF16),
+            pltpu.VMEM((2, 512, 512), BF16),
+            pltpu.VMEM((512, 3 * LANES), BF16),
+            pltpu.VMEM((66 * SLAB, NOBS), BF16),
+            pltpu.VMEM((8, NOBS), F32),
+            pltpu.VMEM((8, NOBS), F32),
             pltpu.SemaphoreType.DMA((NE,)),
             pltpu.SemaphoreType.DMA((NE,)),
             pltpu.SemaphoreType.DMA((NE,)),
@@ -571,12 +615,13 @@
             pltpu.SemaphoreType.DMA((NA * NB,)),
             pltpu.SemaphoreType.DMA((NE,)),
             pltpu.SemaphoreType.DMA((NE,)),
+            pltpu.SemaphoreType.DMA((2,)),
         ],
         compiler_params=pltpu.CompilerParams(
             collective_id=1, has_side_effects=True, vmem_limit_bytes=32 * 1024 * 1024
         ),
         name="cycle",
-    )(x, cw, cb.reshape(1, 256), ow.T, oi, hcol_s, hrow, hcol, obs_r)
+    )(x, cw, cb.reshape(1, 256), ow.T, oi, oc, ov, og, hcol_s, hrow, hcol)
 
 
 def solution(mesh):

time: 76 us -> 68.7 us (0.904)
  Pallas kernels: 72 us -> 65.4 us
    pallas_call x1, Pallas kernels: 60.2 us -> 53.8 us  [per_device(): pl.pallas_call(kernel, out_shape=jax.ShapeDtypeStruct(x.shape, x.dtype),...]
where the time goes in v4:
time: 68.7 us; the launch traced here: 68.5 us
  Pallas kernels  65.4 us (95%)
  local copies, waits for them, and re-layouts  2.37 us (3%)
  between operations  0.75 us (1%)
    pallas_call x1, Pallas kernels, per_device(): pl.pallas_call(kernel, out_shape=jax.ShapeDtypeStruct(x.shape, x.dtype),...  53.8 us
    pallas_call x1, Pallas kernels, per_device(): pl.pallas_call(halo_kernel, out_shape=(jax.ShapeDtypeStruct((2, 2 * NV, L...  11.6 us
    unnamed x17, local copies, waits for them, and re-layouts  2.37 us

profile of v4, /device:TPU:1, one launch (start us, length us, event | category | flops | bytes accessed | tf_op | source)
XLA Modules:
  0.0 68.5 jit_solution(14499943556507549712)
XLA Ops:
  0.7 0.0 copy-start
  0.7 1.0 %copy-done = bf16[1,24,64,128]{3,2,1,0:T(8,128)(2,1)S(1)} copy-done((bf16[1,24,64,128]{3,2,1,0:T(8,128)(2,1)S(1)}, bf16[1,24,64,128]{3,2,1,0:T(8,128)(2,1)}, u32[]{:S(2)}) %copy-start) | copy-done | bytes 393240
  1.6 0.0 copy-start.1
  1.7 0.0 copy-start.2
  1.7 0.0 copy-start.3
  1.7 0.0 copy-start.5
  1.7 0.0 copy-start.6
  1.7 0.0 copy-start.7
  1.7 11.6 %halo.1 = (bf16[2,48,128]{2,1,0:T(8,128)(2,1)S(1)}, bf16[2,48,128]{2,1,0:T(8,128)(2,1)S(1)}, bf16[6,48,128]{2,1,0:T(8,128)(2,1)S(1)}) custom-call(bf16[1,24,64,128]{3,2,1,0:T(8,128)(2,1)S(1)} %copy-done), custom_call_target="tpu_custom_call" | custom-call | flops 10000000000 | bytes 1000000 | tf_op jit(solution)/shard_map/halo/pallas_call | solution.py:558
  13.3 0.0 copy-start.4
  13.3 0.0 copy-done.1
  13.3 0.0 copy-done.2
  13.3 0.0 copy-done.3
  13.3 0.0 copy-done.5
  13.3 0.0 copy-done.6
  13.3 0.0 copy-done.7
  13.4 0.6 copy-done.4
  14.0 53.8 %cycle.1 = bf16[1,24,64,128]{3,2,1,0:T(8,128)(2,1)S(1)} custom-call(bf16[1,24,64,128]{3,2,1,0:T(8,128)(2,1)S(1)} %copy-done.1, bf16[216,256]{1,0:T(8,128)(2,1)S(1)} %copy-done.2, f32[1,256]{1,0:T(1,128)S(1)} %bitcast.3, bf16[24,256]{1,0:T(8,128)(2,1)S(1)} %bitcast.2, s32[1,1,256]{2,1,0:T(1,128)S(1)} %copy-done.5, s32[1,1]{1,0:T(1,128)S(6)} %copy.10.oc, ...), custom_call_target="tpu_custom_call" | custom-call | tf_op jit(solution)/shard_map/cycle/pallas_call | solution.py:581
  67.8 0.7 %copy.11 = bf16[1,24,64,128]{3,2,1,0:T(8,128)(2,1)} copy(bf16[1,24,64,128]{3,2,1,0:T(8,128)(2,1)S(1)} %cycle.1) | data formatting | bytes 786432
Async XLA Ops:
  0.7 1.0 %copy-start = (bf16[1,24,64,128]{3,2,1,0:T(8,128)(2,1)S(1)}, bf16[1,24,64,128]{3,2,1,0:T(8,128)(2,1)}, u32[]{:S(2)}) copy-start(bf16[1,24,64,128]{3,2,1,0:T(8,128)(2,1)} %xv.1) | copy-start | bytes 1179652
  1.6 11.7 %copy-start.1 = (bf16[1,24,64,128]{3,2,1,0:T(8,128)(2,1)S(1)}, bf16[1,24,64,128]{3,2,1,0:T(8,128)(2,1)}, u32[]{:S(2)}) copy-start(bf16[1,24,64,128]{3,2,1,0:T(8,128)(2,1)} %xv.1) | copy-start | bytes 1179652
  1.7 11.7 %copy-start.2 = (bf16[216,256]{1,0:T(8,128)(2,1)S(1)}, bf16[216,256]{1,0:T(8,128)(2,1)}, u32[]{:S(2)}) copy-start(bf16[216,256]{1,0:T(8,128)(2,1)} %cw.1) | copy-start | bytes 331780
  1.7 11.7 %copy-start.3 = (bf16[256,24]{0,1:T(8,128)(2,1)S(1)}, bf16[256,24]{0,1:T(8,128)(2,1)}, u32[]{:S(2)}) copy-start(bf16[256,24]{0,1:T(8,128)(2,1)} %param.11) | copy-start | bytes 36868
  1.7 11.7 %copy-start.5 = (s32[1,1,256]{2,1,0:T(1,128)S(1)}, s32[1,1,256]{2,1,0:T(1,128)}, u32[]{:S(2)}) copy-start(s32[1,1,256]{2,1,0:T(1,128)} %oi.1) | copy-start | bytes 3076
  1.7 11.7 %copy-start.6 = (f32[1,1,256]{2,1,0:T(1,128)S(1)}, f32[1,1,256]{2,1,0:T(1,128)}, u32[]{:S(2)}) copy-start(f32[1,1,256]{2,1,0:T(1,128)} %ov.1) | copy-start | bytes 3076
  1.7 11.7 %copy-start.7 = (f32[1,1,256]{2,1,0:T(1,128)S(1)}, f32[1,1,256]{2,1,0:T(1,128)}, u32[]{:S(2)}) copy-start(f32[1,1,256]{2,1,0:T(1,128)} %og.1) | copy-start | bytes 3076
  13.3 0.7 copy-start.4

commit v5 on v4

--- a/solution.py
+++ b/solution.py
@@ -381,13 +381,6 @@
             t = partner(s)
             f0, f1 = tile(s2, t * 2, q)
             fc[t] = jnp.concatenate([f0, f1], axis=0).astype(BF16)
-            if q:
-                send_tile(s - 1).start()
-
-        @pl.when(outer < 3)
-        def _():
-            send_tile(outer * 8 + 7).start()
-
         return carry
 
     obs_copy = pltpu.make_async_remote_copy(
@@ -397,7 +390,9 @@
     met()
     over(NE, lambda s: send_pick(partner(s)).start())
     obs_copy.start()
-    lax.fori_loop(0, 2, step2, 0)
+    lax.fori_loop(0, 1, step2, 0)
+    over(8, lambda s: send_tile(s).start())
+    lax.fori_loop(1, 4, step2, 0)
 
     def recv_pick(t):
         return pltpu.make_async_remote_copy(
@@ -422,7 +417,13 @@
     packed = jnp.zeros((8, LANES), F32)
     for q in range(4):
         packed = jnp.where(lane8 // 32 == q, g4[8 * q : 8 * q + 8], packed)
-    mine = jnp.concatenate([packed, g4[32:40]], axis=0)
+    row8 = row_iota((8, LANES))
+    spare = (
+        ((row8 == 0) & (lane8 > 1) & (lane8 < NE))
+        | ((row8 == 1) & (lane8 == 0))
+        | ((row8 == 2) & (lane8 == 1))
+    )
+    mine = jnp.where(spare, g4[32:40], packed)
     gsend[...] = mine
     slot = i * NB + j
     grecv[slot] = mine
@@ -444,18 +445,24 @@
     others = [(di, dj) for di in range(NA) for dj in range(NB) if di or dj]
     for di, dj in others:
         send_gram(di, dj).start()
-    lax.fori_loop(2, 4, step2, 0)
+    over(NE - 9, lambda s: send_tile(s + 8).start())
     for di, dj in others:
         recv_gram(di, dj).wait_recv()
 
     total = grecv[0]
     for n in range(1, NA * NB):
         total = total + grecv[n]
-    p1, p2 = total[0:8], total[8:16]
-    gram = jnp.concatenate(
-        [(p1 if q == 0 else roll(p1, -32 * q))[:, 0:32] for q in range(4)], axis=0
-    )
-    proj = p2[:, 0:32]
+    square = jnp.concatenate([roll(total, -32 * q)[:, 0:NE] for q in range(4)], axis=0)
+    row32, lane32 = row_iota((NE, NE)), lane_iota((NE, NE))
+    taken = (
+        ((row32 == 0) & (lane32 > 1))
+        | ((row32 == 1) & (lane32 == 0))
+        | ((row32 == 2) & (lane32 == 1))
+    )
+    gram = jnp.where(taken, square.T, square)
+    lane1 = lane_iota((1, NE))
+    proj = jnp.where(lane1 == 0, square[1:2], jnp.where(lane1 == 1, square[2:3], square[0:1]))
+    proj = jnp.broadcast_to(proj, (8, NE))
     eye = jnp.where(row_iota((NE, NE)) == lane_iota((NE, NE)), 1.0, 0.0)
     system = (NE - 1) * eye + gram
 
@@ -464,11 +471,12 @@
 
     scale = jnp.sqrt(full_sum(system * system))
 
-    current, inverse = system / scale, eye
-    for _ in range(NS_ITERS):
+    current = system / scale
+    inverse = 1.5 * eye - 0.5 * current
+    current = dot(current, inverse, precision=hp)
+    for _ in range(NS_ITERS - 1):
         factor = 1.5 * eye - 0.5 * dot(inverse, current, precision=hp)
-        new = dot(jnp.concatenate([current, inverse], axis=0), factor, precision=hp)
-        current, inverse = new[0:NE], new[NE : 2 * NE]
+        current, inverse = dot(current, factor, precision=hp), dot(factor, inverse, precision=hp)
     root = inverse / jnp.sqrt(scale)
     half = dot(proj, root, precision=hp)
     mean_w = dot(half, root, precision=hp)[0:1]
@@ -595,8 +603,8 @@
             pltpu.VMEM((NE, 2 * NV, LANES), BF16),
             pltpu.VMEM((1, 1, NOBS), F32),
             pltpu.VMEM((NE, 1, NOBS), F32),
-            pltpu.VMEM((16, LANES), F32),
-            pltpu.VMEM((NA * NB, 16, LANES), F32),
+            pltpu.VMEM((8, LANES), F32),
+            pltpu.VMEM((NA * NB, 8, LANES), F32),
             pltpu.VMEM((256, 256), BF16),
             pltpu.VMEM((LANES, NOBS), BF16),
             pltpu.VMEM((NE, 512), BF16),

time: 68.7 us -> 68.2 us (level)
  no operation moved by 1% of the time
where the time goes in v5:
time: 68.2 us; the launch traced here: 68.1 us
  Pallas kernels  64.9 us (95%)
  local copies, waits for them, and re-layouts  2.37 us (3%)
  between operations  0.75 us (1%)
    pallas_call x1, Pallas kernels, per_device(): pl.pallas_call(kernel, out_shape=jax.ShapeDtypeStruct(x.shape, x.dtype),...  53.3 us
    pallas_call x1, Pallas kernels, per_device(): pl.pallas_call(halo_kernel, out_shape=(jax.ShapeDtypeStruct((2, 2 * NV, L...  11.6 us
    unnamed x17, local copies, waits for them, and re-layouts  2.37 us

profile of v5, /device:TPU:1, one launch (start us, length us, event | category | flops | bytes accessed | tf_op | source)
XLA Modules:
  0.0 68.1 jit_solution(14859184190632687568)
XLA Ops:
  0.7 0.0 copy-start
  0.7 1.0 %copy-done = bf16[1,24,64,128]{3,2,1,0:T(8,128)(2,1)S(1)} copy-done((bf16[1,24,64,128]{3,2,1,0:T(8,128)(2,1)S(1)}, bf16[1,24,64,128]{3,2,1,0:T(8,128)(2,1)}, u32[]{:S(2)}) %copy-start) | copy-done | bytes 393240
  1.6 0.0 copy-start.1
  1.7 0.0 copy-start.2
  1.7 0.0 copy-start.3
  1.7 0.0 copy-start.5
  1.7 0.0 copy-start.6
  1.7 0.0 copy-start.7
  1.7 11.6 %halo.1 = (bf16[2,48,128]{2,1,0:T(8,128)(2,1)S(1)}, bf16[2,48,128]{2,1,0:T(8,128)(2,1)S(1)}, bf16[6,48,128]{2,1,0:T(8,128)(2,1)S(1)}) custom-call(bf16[1,24,64,128]{3,2,1,0:T(8,128)(2,1)S(1)} %copy-done), custom_call_target="tpu_custom_call" | custom-call | flops 10000000000 | bytes 1000000 | tf_op jit(solution)/shard_map/halo/pallas_call | solution.py:566
  13.3 0.0 copy-start.4
  13.3 0.0 copy-done.1
  13.3 0.0 copy-done.2
  13.3 0.0 copy-done.3
  13.3 0.0 copy-done.5
  13.3 0.0 copy-done.6
  13.3 0.0 copy-done.7
  13.4 0.6 copy-done.4
  14.0 53.3 %cycle.1 = bf16[1,24,64,128]{3,2,1,0:T(8,128)(2,1)S(1)} custom-call(bf16[1,24,64,128]{3,2,1,0:T(8,128)(2,1)S(1)} %copy-done.1, bf16[216,256]{1,0:T(8,128)(2,1)S(1)} %copy-done.2, f32[1,256]{1,0:T(1,128)S(1)} %bitcast.3, bf16[24,256]{1,0:T(8,128)(2,1)S(1)} %bitcast.2, s32[1,1,256]{2,1,0:T(1,128)S(1)} %copy-done.5, s32[1,1]{1,0:T(1,128)S(6)} %copy.10.oc, ...), custom_call_target="tpu_custom_call" | custom-call | tf_op jit(solution)/shard_map/cycle/pallas_call | solution.py:589
  67.3 0.7 %copy.11 = bf16[1,24,64,128]{3,2,1,0:T(8,128)(2,1)} copy(bf16[1,24,64,128]{3,2,1,0:T(8,128)(2,1)S(1)} %cycle.1) | data formatting | bytes 786432
Async XLA Ops:
  0.7 1.0 %copy-start = (bf16[1,24,64,128]{3,2,1,0:T(8,128)(2,1)S(1)}, bf16[1,24,64,128]{3,2,1,0:T(8,128)(2,1)}, u32[]{:S(2)}) copy-start(bf16[1,24,64,128]{3,2,1,0:T(8,128)(2,1)} %xv.1) | copy-start | bytes 1179652
  1.6 11.7 %copy-start.1 = (bf16[1,24,64,128]{3,2,1,0:T(8,128)(2,1)S(1)}, bf16[1,24,64,128]{3,2,1,0:T(8,128)(2,1)}, u32[]{:S(2)}) copy-start(bf16[1,24,64,128]{3,2,1,0:T(8,128)(2,1)} %xv.1) | copy-start | bytes 1179652
  1.7 11.7 %copy-start.2 = (bf16[216,256]{1,0:T(8,128)(2,1)S(1)}, bf16[216,256]{1,0:T(8,128)(2,1)}, u32[]{:S(2)}) copy-start(bf16[216,256]{1,0:T(8,128)(2,1)} %cw.1) | copy-start | bytes 331780
  1.7 11.7 %copy-start.3 = (bf16[256,24]{0,1:T(8,128)(2,1)S(1)}, bf16[256,24]{0,1:T(8,128)(2,1)}, u32[]{:S(2)}) copy-start(bf16[256,24]{0,1:T(8,128)(2,1)} %param.11) | copy-start | bytes 36868
  1.7 11.7 %copy-start.5 = (s32[1,1,256]{2,1,0:T(1,128)S(1)}, s32[1,1,256]{2,1,0:T(1,128)}, u32[]{:S(2)}) copy-start(s32[1,1,256]{2,1,0:T(1,128)} %oi.1) | copy-start | bytes 3076
  1.7 11.7 %copy-start.6 = (f32[1,1,256]{2,1,0:T(1,128)S(1)}, f32[1,1,256]{2,1,0:T(1,128)}, u32[]{:S(2)}) copy-start(f32[1,1,256]{2,1,0:T(1,128)} %ov.1) | copy-start | bytes 3076
  1.7 11.7 %copy-start.7 = (f32[1,1,256]{2,1,0:T(1,128)S(1)}, f32[1,1,256]{2,1,0:T(1,128)}, u32[]{:S(2)}) copy-start(f32[1,1,256]{2,1,0:T(1,128)} %og.1) | copy-start | bytes 3076
  13.3 0.7 %copy-start.4 = (f32[256]{0:T(256)S(1)}, f32[256]{0:T(256)}, u32[]{:S(2)}) copy-start(f32[256]{0:T(256)} %param.10) | copy-start | bytes 3076

commit v6 on v5

--- a/solution.py
+++ b/solution.py
@@ -79,7 +79,10 @@
     j = lax.axis_index("lon")
 
     def peer(dk, di, dj):
-        return ((k + dk) % NE, (i + di) % NA, (j + dj) % NB)
+        return tuple(
+            at if d % n == 0 else lax.rem(at + d % n, n)
+            for at, d, n in ((k, dk, NE), (i, di, NA), (j, dj, NB))
+        )
 
     return k, i, j, peer
 
@@ -201,30 +204,43 @@
     asend, arecv, psend, precv, gsend_sem, grecv_sem, bsend, brecv, osem,
 ):
     k, i, j, peer = place()
-    i2 = (i + 2) % NA
-    k_hi, k_y, k_c = k // 16, (k // 2) % 8, k % 2
+    i2 = lax.rem(i + 2, NA)
+    k_hi, k_y, k_c = lax.div(k, 16), lax.rem(lax.div(k, 2), 8), lax.rem(k, 2)
 
     def partner(s):
+        s = lax.rem(s + 1, NE)
+        u = lax.div(s, 4)
+        dy = lax.div(u + 1, 2) * (2 * lax.rem(u, 2) - 1)
+        hi = lax.rem(k_hi + s, 2)
+        y = lax.rem(k_y + 8 + dy, 8)
+        c = lax.rem(k_c + lax.div(s, 2), 2)
+        return hi * 16 + y * 2 + c
+
+    met = meet(
+        [peer(0, di, dj) for di in range(NA) for dj in range(NB) if di or dj]
+        + [peer(dk, di, 0) for dk in range(1, NE) for di in (0, 2)]
+    )
+    lane24 = lane_iota((NV, LANES))
+    fill(big, xv)
+
+    def row_of(r):
+        return big[pl.ds(r, NV, stride=PITCH), :]
+
+    def over(n, body):
+        lax.fori_loop(0, n, lambda s, c: (body(s), c)[1], 0)
+
+    def each(start, stop, body):
+        for s in range(start, stop):
+            body(toward(s))
+
+    def toward(s):
         s = (s + 1) % NE
         u = s // 4
         dy = ((u + 1) // 2) * (2 * (u % 2) - 1)
-        hi = (k_hi + s) % 2
-        y = (k_y + 8 + dy) % 8
-        c = (k_c + s // 2) % 2
+        hi = 1 - k_hi if s % 2 else k_hi
+        y = lax.rem(k_y + (8 + dy) % 8, 8)
+        c = 1 - k_c if (s // 2) % 2 else k_c
         return hi * 16 + y * 2 + c
-
-    met = meet(
-        [peer(0, di, dj) for di in range(NA) for dj in range(NB) if di or dj]
-        + [peer(dk, di, 0) for dk in range(1, NE) for di in (0, 2)]
-    )
-    lane24 = lane_iota((NV, LANES))
-    fill(big, xv)
-
-    def row_of(r):
-        return big[pl.ds(r, NV, stride=PITCH), :]
-
-    def over(n, body):
-        lax.fori_loop(0, n, lambda s, c: (body(s), c)[1], 0)
 
     w = cw[...].astype(F32)
     b = cb[...]
@@ -366,8 +382,7 @@
             device_id=(t, i2, j), device_id_type=MESH,
         )
 
-    def send_tile(s):
-        t = partner(s)
+    def send_tile(t):
         return pltpu.make_async_remote_copy(
             src_ref=fc.at[t], dst_ref=recv.at[k], send_sem=asend.at[t], recv_sem=arecv.at[k],
             device_id=(t, i, j), device_id_type=MESH,
@@ -388,10 +403,10 @@
         device_id=(k, i2, j), device_id_type=MESH,
     )
     met()
-    over(NE, lambda s: send_pick(partner(s)).start())
+    each(0, NE, lambda t: send_pick(t).start())
     obs_copy.start()
     lax.fori_loop(0, 1, step2, 0)
-    over(8, lambda s: send_tile(s).start())
+    each(0, 8, lambda t: send_tile(t).start())
     lax.fori_loop(1, 4, step2, 0)
 
     def recv_pick(t):
@@ -445,7 +460,7 @@
     others = [(di, dj) for di in range(NA) for dj in range(NB) if di or dj]
     for di, dj in others:
         send_gram(di, dj).start()
-    over(NE - 9, lambda s: send_tile(s + 8).start())
+    each(8, NE - 1, lambda t: send_tile(t).start())
     for di, dj in others:
         recv_gram(di, dj).wait_recv()
 
@@ -505,7 +520,7 @@
         )
 
     recv[k] = fc[k]
-    over(NE - 1, lambda s: recv_tile(partner(s)).wait_recv())
+    each(0, NE - 1, lambda t: recv_tile(t).wait_recv())
 
     for q in range(3):
         fr[:, q * LANES : (q + 1) * LANES] = recv[:, 16 * q : 16 * q + 16, :].reshape(512, LANES)
@@ -523,11 +538,11 @@
         )
 
     def group(g):
-        return (k // 8 + 1 + g) % 4
+        return lax.rem(lax.div(k, 8) + 1 + g, 4)
 
     def send_group(g):
         for e in range(8 if g < 3 else 7):
-            send_back(group(g) * 8 + (k + 1 + e) % 8).start()
+            send_back(group(g) * 8 + lax.rem(k + 1 + e, 8)).start()
 
     for g in range(4):
         rows = pl.ds(pl.multiple_of(group(g) * LANES, LANES), LANES)

time: 68.2 us -> 66 us (0.968)
  Pallas kernels: 64.9 us -> 62.7 us
    pallas_call x1, Pallas kernels: 53.3 us -> 51.1 us  [per_device(): pl.pallas_call(kernel, out_shape=jax.ShapeDtypeStruct(x.shape, x.dtype),...]
where the time goes in v6:
time: 66 us; the launch traced here: 65.8 us
  Pallas kernels  62.7 us (95%)
  local copies, waits for them, and re-layouts  2.37 us (4%)
  between operations  0.75 us (1%)
    pallas_call x1, Pallas kernels, per_device(): pl.pallas_call(kernel, out_shape=jax.ShapeDtypeStruct(x.shape, x.dtype),...  51.1 us
    pallas_call x1, Pallas kernels, per_device(): pl.pallas_call(halo_kernel, out_shape=(jax.ShapeDtypeStruct((2, 2 * NV, L...  11.6 us
    unnamed x17, local copies, waits for them, and re-layouts  2.37 us

profile of v6, /device:TPU:1, one launch (start us, length us, event | category | flops | bytes accessed | tf_op | source)
XLA Modules:
  0.0 65.8 jit_solution(4607341994024738270)
XLA Ops:
  0.7 0.0 copy-start
  0.7 1.0 %copy-done = bf16[1,24,64,128]{3,2,1,0:T(8,128)(2,1)S(1)} copy-done((bf16[1,24,64,128]{3,2,1,0:T(8,128)(2,1)S(1)}, bf16[1,24,64,128]{3,2,1,0:T(8,128)(2,1)}, u32[]{:S(2)}) %copy-start) | copy-done | bytes 393240
  1.6 0.0 copy-start.1
  1.7 0.0 copy-start.2
  1.7 0.0 copy-start.3
  1.7 0.0 copy-start.5
  1.7 0.0 copy-start.6
  1.7 0.0 copy-start.7
  1.7 11.6 %halo.1 = (bf16[2,48,128]{2,1,0:T(8,128)(2,1)S(1)}, bf16[2,48,128]{2,1,0:T(8,128)(2,1)S(1)}, bf16[6,48,128]{2,1,0:T(8,128)(2,1)S(1)}) custom-call(bf16[1,24,64,128]{3,2,1,0:T(8,128)(2,1)S(1)} %copy-done), custom_call_target="tpu_custom_call" | custom-call | flops 10000000000 | bytes 1000000 | tf_op jit(solution)/shard_map/halo/pallas_call | solution.py:581
  13.3 0.0 copy-start.4
  13.3 0.0 copy-done.1
  13.3 0.0 copy-done.2
  13.3 0.0 copy-done.3
  13.3 0.0 copy-done.5
  13.3 0.0 copy-done.6
  13.3 0.0 copy-done.7
  13.3 0.6 copy-done.4
  14.0 51.1 %cycle.1 = bf16[1,24,64,128]{3,2,1,0:T(8,128)(2,1)S(1)} custom-call(bf16[1,24,64,128]{3,2,1,0:T(8,128)(2,1)S(1)} %copy-done.1, bf16[216,256]{1,0:T(8,128)(2,1)S(1)} %copy-done.2, f32[1,256]{1,0:T(1,128)S(1)} %bitcast.3, bf16[24,256]{1,0:T(8,128)(2,1)S(1)} %bitcast.2, s32[1,1,256]{2,1,0:T(1,128)S(1)} %copy-done.5, s32[1,1]{1,0:T(1,128)S(6)} %copy.10.oc, ...), custom_call_target="tpu_custom_call" | custom-call | tf_op jit(solution)/shard_map/cycle/pallas_call | solution.py:604
  65.1 0.7 %copy.11 = bf16[1,24,64,128]{3,2,1,0:T(8,128)(2,1)} copy(bf16[1,24,64,128]{3,2,1,0:T(8,128)(2,1)S(1)} %cycle.1) | data formatting | bytes 786432
Async XLA Ops:
  0.7 1.0 %copy-start = (bf16[1,24,64,128]{3,2,1,0:T(8,128)(2,1)S(1)}, bf16[1,24,64,128]{3,2,1,0:T(8,128)(2,1)}, u32[]{:S(2)}) copy-start(bf16[1,24,64,128]{3,2,1,0:T(8,128)(2,1)} %xv.1) | copy-start | bytes 1179652
  1.6 11.6 %copy-start.1 = (bf16[1,24,64,128]{3,2,1,0:T(8,128)(2,1)S(1)}, bf16[1,24,64,128]{3,2,1,0:T(8,128)(2,1)}, u32[]{:S(2)}) copy-start(bf16[1,24,64,128]{3,2,1,0:T(8,128)(2,1)} %xv.1) | copy-start | bytes 1179652
  1.7 11.6 %copy-start.2 = (bf16[216,256]{1,0:T(8,128)(2,1)S(1)}, bf16[216,256]{1,0:T(8,128)(2,1)}, u32[]{:S(2)}) copy-start(bf16[216,256]{1,0:T(8,128)(2,1)} %cw.1) | copy-start | bytes 331780
  1.7 11.7 %copy-start.3 = (bf16[256,24]{0,1:T(8,128)(2,1)S(1)}, bf16[256,24]{0,1:T(8,128)(2,1)}, u32[]{:S(2)}) copy-start(bf16[256,24]{0,1:T(8,128)(2,1)} %param.11) | copy-start | bytes 36868
  1.7 11.7 %copy-start.5 = (s32[1,1,256]{2,1,0:T(1,128)S(1)}, s32[1,1,256]{2,1,0:T(1,128)}, u32[]{:S(2)}) copy-start(s32[1,1,256]{2,1,0:T(1,128)} %oi.1) | copy-start | bytes 3076
  1.7 11.7 %copy-start.6 = (f32[1,1,256]{2,1,0:T(1,128)S(1)}, f32[1,1,256]{2,1,0:T(1,128)}, u32[]{:S(2)}) copy-start(f32[1,1,256]{2,1,0:T(1,128)} %ov.1) | copy-start | bytes 3076
  1.7 11.7 %copy-start.7 = (f32[1,1,256]{2,1,0:T(1,128)S(1)}, f32[1,1,256]{2,1,0:T(1,128)}, u32[]{:S(2)}) copy-start(f32[1,1,256]{2,1,0:T(1,128)} %og.1) | copy-start | bytes 3076
  13.3 0.7 %copy-start.4 = (f32[256]{0:T(256)S(1)}, f32[256]{0:T(256)}, u32[]{:S(2)}) copy-start(f32[256]{0:T(256)} %param.10) | copy-start | bytes 3076

commit v7 on v6

--- a/solution.py
+++ b/solution.py
@@ -570,8 +570,8 @@
         out_ref[0, v] = big[pl.ds(v, ROWS, stride=NV), :].astype(BF16)
 
     over(NE, lambda t: recv_pick(t).wait_send())
-    over(NE - 1, lambda s: recv_tile(partner(s)).wait_send())
-    over(NE - 1, lambda s: recv_back(partner(s)).wait_send())
+    each(0, NE - 1, lambda t: recv_tile(t).wait_send())
+    each(0, NE - 1, lambda t: recv_back(t).wait_send())
     for di, dj in others:
         send_gram(di, dj).wait_send()
 

time: 66 us -> 64.8 us (0.982)
  Pallas kernels: 62.7 us -> 61.5 us
    pallas_call x1, Pallas kernels: 51.1 us -> 49.9 us  [per_device(): pl.pallas_call(kernel, out_shape=jax.ShapeDtypeStruct(x.shape, x.dtype),...]
where the time goes in v7:
time: 64.8 us; the launch traced here: 64.6 us
  Pallas kernels  61.5 us (95%)
  local copies, waits for them, and re-layouts  2.37 us (4%)
  between operations  0.75 us (1%)
    pallas_call x1, Pallas kernels, per_device(): pl.pallas_call(kernel, out_shape=jax.ShapeDtypeStruct(x.shape, x.dtype),...  49.9 us
    pallas_call x1, Pallas kernels, per_device(): pl.pallas_call(halo_kernel, out_shape=(jax.ShapeDtypeStruct((2, 2 * NV, L...  11.6 us
    unnamed x17, local copies, waits for them, and re-layouts  2.37 us

profile of v7, /device:TPU:1, one launch (start us, length us, event | category | flops | bytes accessed | tf_op | source)
XLA Modules:
  0.0 64.6 jit_solution(11574133205979170010)
XLA Ops:
  0.7 0.0 copy-start
  0.7 1.0 %copy-done = bf16[1,24,64,128]{3,2,1,0:T(8,128)(2,1)S(1)} copy-done((bf16[1,24,64,128]{3,2,1,0:T(8,128)(2,1)S(1)}, bf16[1,24,64,128]{3,2,1,0:T(8,128)(2,1)}, u32[]{:S(2)}) %copy-start) | copy-done | bytes 393240
  1.6 0.0 copy-start.1
  1.7 0.0 copy-start.2
  1.7 0.0 copy-start.3
  1.7 0.0 copy-start.5
  1.7 0.0 copy-start.6
  1.7 0.0 copy-start.7
  1.7 11.6 %halo.1 = (bf16[2,48,128]{2,1,0:T(8,128)(2,1)S(1)}, bf16[2,48,128]{2,1,0:T(8,128)(2,1)S(1)}, bf16[6,48,128]{2,1,0:T(8,128)(2,1)S(1)}) custom-call(bf16[1,24,64,128]{3,2,1,0:T(8,128)(2,1)S(1)} %copy-done), custom_call_target="tpu_custom_call" | custom-call | flops 10000000000 | bytes 1000000 | tf_op jit(solution)/shard_map/halo/pallas_call | solution.py:581
  13.3 0.0 copy-start.4
  13.3 0.0 copy-done.1
  13.3 0.0 copy-done.2
  13.3 0.0 copy-done.3
  13.3 0.0 copy-done.5
  13.3 0.0 copy-done.6
  13.3 0.0 copy-done.7
  13.3 0.6 copy-done.4
  14.0 49.9 %cycle.1 = bf16[1,24,64,128]{3,2,1,0:T(8,128)(2,1)S(1)} custom-call(bf16[1,24,64,128]{3,2,1,0:T(8,128)(2,1)S(1)} %copy-done.1, bf16[216,256]{1,0:T(8,128)(2,1)S(1)} %copy-done.2, f32[1,256]{1,0:T(1,128)S(1)} %bitcast.3, bf16[24,256]{1,0:T(8,128)(2,1)S(1)} %bitcast.2, s32[1,1,256]{2,1,0:T(1,128)S(1)} %copy-done.5, s32[1,1]{1,0:T(1,128)S(6)} %copy.10.oc, ...), custom_call_target="tpu_custom_call" | custom-call | tf_op jit(solution)/shard_map/cycle/pallas_call | solution.py:604
  63.8 0.7 %copy.11 = bf16[1,24,64,128]{3,2,1,0:T(8,128)(2,1)} copy(bf16[1,24,64,128]{3,2,1,0:T(8,128)(2,1)S(1)} %cycle.1) | data formatting | bytes 786432
Async XLA Ops:
  0.7 1.0 %copy-start = (bf16[1,24,64,128]{3,2,1,0:T(8,128)(2,1)S(1)}, bf16[1,24,64,128]{3,2,1,0:T(8,128)(2,1)}, u32[]{:S(2)}) copy-start(bf16[1,24,64,128]{3,2,1,0:T(8,128)(2,1)} %xv.1) | copy-start | bytes 1179652
  1.6 11.6 %copy-start.1 = (bf16[1,24,64,128]{3,2,1,0:T(8,128)(2,1)S(1)}, bf16[1,24,64,128]{3,2,1,0:T(8,128)(2,1)}, u32[]{:S(2)}) copy-start(bf16[1,24,64,128]{3,2,1,0:T(8,128)(2,1)} %xv.1) | copy-start | bytes 1179652
  1.7 11.6 %copy-start.2 = (bf16[216,256]{1,0:T(8,128)(2,1)S(1)}, bf16[216,256]{1,0:T(8,128)(2,1)}, u32[]{:S(2)}) copy-start(bf16[216,256]{1,0:T(8,128)(2,1)} %cw.1) | copy-start | bytes 331780
  1.7 11.7 %copy-start.3 = (bf16[256,24]{0,1:T(8,128)(2,1)S(1)}, bf16[256,24]{0,1:T(8,128)(2,1)}, u32[]{:S(2)}) copy-start(bf16[256,24]{0,1:T(8,128)(2,1)} %param.11) | copy-start | bytes 36868
  1.7 11.7 %copy-start.5 = (s32[1,1,256]{2,1,0:T(1,128)S(1)}, s32[1,1,256]{2,1,0:T(1,128)}, u32[]{:S(2)}) copy-start(s32[1,1,256]{2,1,0:T(1,128)} %oi.1) | copy-start | bytes 3076
  1.7 11.7 %copy-start.6 = (f32[1,1,256]{2,1,0:T(1,128)S(1)}, f32[1,1,256]{2,1,0:T(1,128)}, u32[]{:S(2)}) copy-start(f32[1,1,256]{2,1,0:T(1,128)} %ov.1) | copy-start | bytes 3076
  1.7 11.7 %copy-start.7 = (f32[1,1,256]{2,1,0:T(1,128)S(1)}, f32[1,1,256]{2,1,0:T(1,128)}, u32[]{:S(2)}) copy-start(f32[1,1,256]{2,1,0:T(1,128)} %og.1) | copy-start | bytes 3076
  13.3 0.7 %copy-start.4 = (f32[256]{0:T(256)S(1)}, f32[256]{0:T(256)}, u32[]{:S(2)}) copy-start(f32[256]{0:T(256)} %param.10) | copy-start | bytes 3076
